TPU v7x, 256 devices: a whole 4x4x8 slice. The times are simulated.
256 devices in a mesh: rows: 32 (over y, x, core), feat: 8 (over z).
Axes of the slice: x: 4, y: 4, z: 8, core: 2. Of those that a mesh axis runs over, the one named last changes fastest.
Arguments:
- features: bfloat16 [32768, 2048], P('rows', 'feat'), may hold values from -6 to 6
- grad_out: bfloat16 [32768, 2048], P('rows', 'feat'), may hold values from -6 to 6
- eigvecs: float32 [2048, 2048], P('feat', 'rows'), may hold values from -1 to 1, as said below
- eigvals: float32 [2048], replicated, may hold values from 0.1 to 1, as said below
- whiten: bfloat16 [2048, 2048], P(None, 'feat'), may hold values from -0.125 to 0.125
Outputs:
- grad_in: bfloat16 [32768, 2048], P('rows', 'feat')
Inputs may be any that keep to these rules, and one draw needn't show every extreme that they name: `eigvecs`: the columns are orthonormal. `eigvals`: any two entries differ by at least 0.45 / 2048.
All inputs are finite; a program needn't handle non-finite values.
Results may differ from a plain program's by a relative error of at most 0.0074.
Values may be sent and summed in bfloat16 or wider, within the bound.
A program may use at most 128 MiB of HBM per device.

v0:
```python
import functools

import jax
import jax.numpy as jnp
from jax import lax
from jax.experimental import pallas as pl
from jax.experimental.pallas import tpu as pltpu
from jax.sharding import PartitionSpec as P

MESH = pl.DeviceIdType.MESH
VMEM = pl.BlockSpec(memory_space=pltpu.VMEM)
bf16, f32 = jnp.bfloat16, jnp.float32


def peer(axis, index):
    return {axis: index}


def greet(axis, targets):
    barrier = pltpu.get_barrier_semaphore()
    for target in targets:
        pl.semaphore_signal(barrier, inc=1, device_id=peer(axis, target), device_id_type=MESH)
    pl.semaphore_wait(barrier, len(targets))


def remote(src, dst, send, recv, axis, target):
    return pltpu.make_async_remote_copy(
        src_ref=src, dst_ref=dst, send_sem=send, recv_sem=recv,
        device_id=peer(axis, target), device_id_type=MESH,
    )


def exchange_kernel(axis, n, same, x_ref, o_ref, send, recv):
    me = lax.axis_index(axis)
    targets = [lax.rem(me + d, n) for d in range(1, n)]
    greet(axis, targets)
    copies = []
    for d in range(1, n):
        src = x_ref if same else x_ref.at[targets[d - 1]]
        copy = remote(src, o_ref.at[me], send.at[d - 1], recv.at[d - 1], axis, targets[d - 1])
        copy.start()
        copies.append(copy)
    o_ref[me] = x_ref[...] if same else x_ref[me]
    for copy in copies:
        copy.wait()


def gather_kernel(axis, n, x_ref, o_ref, send, recv, core_send, core_recv):
    me = lax.axis_index(axis)
    core = lax.rem(me, 2)
    mate = me + 1 - 2 * core
    h = n // 2
    targets = [lax.rem(me + 2 * d, n) for d in range(1, h)]
    greet(axis, [mate] + targets)
    copies = []
    for d in range(1, h):
        copy = remote(x_ref, o_ref.at[me], send.at[d], recv.at[d], axis, targets[d - 1])
        copy.start()
        copies.append(copy)
    passed = [remote(x_ref, o_ref.at[me], core_send.at[0], core_recv.at[0], axis, mate)]
    passed[0].start()
    o_ref[me] = x_ref[...]
    for d in range(1, h):
        source = lax.rem(me + n - 2 * d, n)
        copies[d - 1].wait_recv()
        copy = remote(o_ref.at[source], o_ref.at[source], core_send.at[d], core_recv.at[d], axis, mate)
        copy.start()
        passed.append(copy)
    for copy in copies:
        copy.wait_send()
    for copy in passed:
        copy.wait()


def scatter_kernel(axis, n, x_ref, o_ref, landed, stage, parts, send, recv, core_send, core_recv):
    me = lax.axis_index(axis)
    core = lax.rem(me, 2)
    chip = me // 2
    mate = me + 1 - 2 * core
    h = n // 2
    targets = [lax.rem(me + 2 * d, n) for d in range(1, h)]
    greet(axis, [mate] + targets)
    core_copies = []
    for d in list(range(1, h)) + [0]:
        there = lax.rem(chip + d, h)
        copy = remote(x_ref.at[1 - core, there], landed.at[d], core_send.at[d], core_recv.at[d], axis, mate)
        copy.start()
        core_copies.append(copy)
    copies = []
    for order, d in enumerate(range(1, h)):
        there = lax.rem(chip + d, h)
        core_copies[order].wait_recv()
        stage[d - 1] = (x_ref[core, there].astype(f32) + landed[d].astype(f32)).astype(bf16)
        copy = remote(stage.at[d - 1], parts.at[d - 1], send.at[d - 1], recv.at[d - 1], axis, targets[d - 1])
        copy.start()
        copies.append(copy)
    core_copies[-1].wait_recv()
    total = x_ref[core, chip].astype(f32) + landed[0].astype(f32)
    for d in range(1, h):
        copies[d - 1].wait_recv()
        total = total + parts[d - 1].astype(f32)
    o_ref[...] = total.astype(bf16)
    for copy in copies + core_copies:
        copy.wait_send()


def call(kernel, out, scratch, cid, sent, *args):
    return pl.pallas_call(
        kernel,
        out_shape=out,
        in_specs=[VMEM] * len(args),
        out_specs=jax.tree.map(lambda _: VMEM, out),
        scratch_shapes=scratch,
        compiler_params=pltpu.CompilerParams(collective_id=cid, has_side_effects=True, vmem_limit_bytes=48 * 2**20),
        cost_estimate=pl.CostEstimate(flops=8_000_000_000, bytes_accessed=sent, transcendentals=0),
    )(*args)


def exchange(x, axis, cid, same=False):
    n = lax.axis_size(axis)
    shape = (n,) + x.shape if same else x.shape
    sems = [pltpu.SemaphoreType.DMA((n - 1,))] * 2
    return call(functools.partial(exchange_kernel, axis, n, same), jax.ShapeDtypeStruct(shape, x.dtype), sems, cid, x.nbytes, x)


def gather(x, axis, cid):
    n = lax.axis_size(axis)
    sems = [pltpu.SemaphoreType.DMA((n // 2,))] * 4
    return call(functools.partial(gather_kernel, axis, n), jax.ShapeDtypeStruct((n,) + x.shape, x.dtype), sems, cid, x.nbytes, x)


def scatter(x, axis, cid):
    n = lax.axis_size(axis)
    h, piece = n // 2, x.shape[2:]
    scratch = [pltpu.VMEM((h,) + piece, bf16), pltpu.VMEM((h,) + piece, bf16), pltpu.VMEM((h,) + piece, bf16)]
    scratch += [pltpu.SemaphoreType.DMA((h,))] * 4
    return call(functools.partial(scatter_kernel, axis, n), jax.ShapeDtypeStruct(piece, bf16), scratch, cid, x.nbytes, x)


def lanes(index, width):
    return pl.ds(pl.multiple_of(index * width, width), width)


def chain_kernel(n, zn, chunks, scale, x_ref, v_ref, k_ref, f_ref, o_ref, f_out, landed, stage, parts, c_col, turned, rows,
                 t_out, t_in, spread, n_out, n_in, own_q, rs, zs, ss, ts, ns, gs, fs):
    me, z = lax.axis_index("rows"), lax.axis_index("feat")
    core, chip = lax.rem(me, 2), me // 2
    mate = me + 1 - 2 * core
    h, per = n // 2, n // zn
    nar = t_out.shape[1]
    own = x_ref.shape[0]
    barrier = pltpu.get_barrier_semaphore()
    for d in range(1, n):
        pl.semaphore_signal(barrier, inc=1, device_id={"rows": lax.rem(me + d, n)}, device_id_type=MESH)
    for d in range(1, zn):
        pl.semaphore_signal(barrier, inc=1, device_id={"feat": lax.rem(z + d, zn)}, device_id_type=MESH)
    pl.semaphore_wait(barrier, n + zn - 2)
    ck = f_ref.shape[0] // chunks

    def hop(way, step, unit):
        there = f_out.at[pl.ds(unit * ck, ck), lanes(z - step if way == 0 else z + step, own)]
        src = there if step else f_ref.at[pl.ds(unit * ck, ck)]
        target = lax.rem(z + (1 if way == 0 else zn - 1), zn)
        return remote(src, there, fs[0].at[way, step, unit], fs[1].at[way, step, unit], "feat", target)

    def held(way, step):
        return z >= step if way == 0 else z + step < zn

    def onward(way):
        return z < zn - 1 if way == 0 else z > 0

    def forward(step, some):
        for unit in some:
            for way in (0, 1):
                @pl.when(held(way, step))
                def _():
                    hop(way, step - 1, unit).wait_recv()
                    if step < zn - 1:
                        @pl.when(onward(way))
                        def _():
                            hop(way, step, unit).start()

    every = range(chunks)

    def begin(some):
        for unit in some:
            for way in (0, 1):
                @pl.when(onward(way))
                def _():
                    hop(way, 0, unit).start()

    begin(every[: chunks // 2])
    f_out[:, lanes(z, own)] = f_ref[...]

    pending = []
    core_copies = []
    order = list(range(1, h)) + [0]
    for d in order:
        piece = 2 * lax.rem(chip + d, h) + 1 - core
        copy = remote(x_ref.at[:, lanes(piece, nar)], landed.at[d], rs[0].at[d], rs[1].at[d], "rows", mate)
        copy.start()
        core_copies.append(copy)
    copies = []
    for i, d in enumerate(order):
        piece = 2 * lax.rem(chip + d, h) + core
        core_copies[i].wait_recv()
        both = x_ref[:, lanes(piece, nar)].astype(f32) + landed[d].astype(f32)
        if d:
            stage[d] = both.astype(bf16)
            copy = remote(stage.at[d], parts.at[d], rs[2].at[d], rs[3].at[d], "rows", lax.rem(me + 2 * d, n))
            copy.start()
            copies.append(copy)
    for d in range(1, h):
        copies[d - 1].wait_recv()
        both = both + parts[d].astype(f32)
    c_col[z] = both.astype(bf16)
    pending += core_copies + copies

    def pass_tiles(block):
        for i in range(per):
            s = block * per + i
            off = lax.rem(s - me + n, n)

            @pl.when(off != 0)
            def _():
                remote(c_col.at[block, pl.ds(i * nar, nar)], turned.at[me], ss[0].at[off - 1], ss[1].at[off - 1], "rows", s).start()

            @pl.when(off == 0)
            def _():
                turned[me] = c_col[block, pl.ds(i * nar, nar)]

    z_copies = []
    for d in range(1, zn):
        copy = remote(c_col.at[z], c_col.at[z], zs[0].at[d - 1], zs[1].at[d - 1], "feat", lax.rem(z + d, zn))
        copy.start()
        z_copies.append(copy)
    begin(every[chunks // 2 :])
    pass_tiles(z)
    for d in range(1, zn):
        z_copies[d - 1].wait_recv()
        pass_tiles(lax.rem(z + zn - d, zn))
    pending += z_copies
    forward(1, every)

    def add_rows(source):
        inner = c_col[source // per, pl.ds(pl.multiple_of(lax.rem(source, per) * nar, nar), nar)]
        both = 0.5 * (turned[source].astype(f32) + inner.astype(f32).T)
        rows[:, lanes(source, nar)] = both.astype(bf16)

    for d in range(n):
        source = lax.rem(me + n - d, n)
        if d:
            copy = remote(c_col.at[0, pl.ds(0, nar)], turned.at[source], ss[0].at[d - 1], ss[1].at[d - 1], "rows", lax.rem(me + d, n))
            copy.wait_recv()
            pending.append(copy)
        add_rows(source)

    def swap(make, outs, ins, sems):
        copies = []
        for d in list(range(1, n)) + [0]:
            s = lax.rem(me + d, n)
            piece = make(s).astype(bf16)
            if d:
                outs[s] = piece
                copy = remote(outs.at[s], ins.at[me], sems[0].at[d - 1], sems[1].at[d - 1], "rows", s)
                copy.start()
                copies.append(copy)
            else:
                ins[me] = piece
        return copies

    half = zn // 2
    for step in range(2, half):
        forward(step, every)
    t_copies = swap(lambda s: jnp.dot(rows[...], v_ref[s], preferred_element_type=f32), t_out, t_in, ts)
    for d in range(n):
        source = lax.rem(me + n - d, n)
        if d:
            t_copies[d - 1].wait_recv()
        spread[:, lanes(source, nar)] = t_in[source].astype(f32).T.astype(bf16)
    pending += t_copies
    if half > 1:
        forward(half, every[: chunks // 2])
    for q in range(n):
        block = jnp.dot(spread[...], v_ref[q], preferred_element_type=f32)
        rows[:, pl.ds(q * nar, nar)] = (k_ref[:, pl.ds(q * nar, nar)] * block).astype(bf16)

    def back(s):
        total = None
        for q in range(n):
            term = lax.dot_general(
                rows[:, pl.ds(q * nar, nar)], v_ref[q, pl.ds(pl.multiple_of(s * nar, nar), nar)],
                (((1,), (1,)), ((), ())), preferred_element_type=f32,
            )
            total = term if total is None else total + term
        return total

    n_copies = swap(back, n_out, n_in, ns)
    pending += n_copies
    if half > 1:
        forward(half, every[chunks // 2 :])
    total = None
    for d in range(n):
        source = lax.rem(me + n - d, n)
        if d:
            n_copies[d - 1].wait_recv()
        left = v_ref[source, pl.ds(pl.multiple_of(z * own, own), own)]
        term = jnp.dot(left, n_in[source], preferred_element_type=f32)
        total = term if total is None else total + term
    own_q[...] = (scale * total).astype(bf16)

    copies, passed = [], []
    mine = o_ref.at[:, lanes(me, nar)]
    for d in range(1, h):
        copy = remote(own_q, mine, gs[0].at[d], gs[1].at[d], "rows", lax.rem(me + 2 * d, n))
        copy.start()
        copies.append(copy)
    passed.append(remote(own_q, mine, gs[2].at[0], gs[3].at[0], "rows", mate))
    passed[0].start()
    o_ref[:, lanes(me, nar)] = own_q[...]
    for d in range(1, h):
        there = o_ref.at[:, lanes(lax.rem(me + n - 2 * d, n), nar)]
        copies[d - 1].wait_recv()
        copy = remote(there, there, gs[2].at[d], gs[3].at[d], "rows", mate)
        copy.start()
        passed.append(copy)
    for step in range(max(half, 1) + 1, zn):
        forward(step, every)
    for copy in passed:
        copy.wait()
    for copy in copies + pending:
        copy.wait_send()
    for step in range(zn - 1):
        for unit in every:
            for way in (0, 1):
                @pl.when(jnp.logical_and(held(way, step), onward(way)))
                def _():
                    hop(way, step, unit).wait_send()


def chain(part, v_pieces, kernel_rows, x, row_count):
    n, zn = lax.axis_size("rows"), lax.axis_size("feat")
    own, d_all = part.shape
    nar, h = d_all // n, n // 2
    tile, square = (h, own, nar), (n, nar, nar)
    dma = pltpu.SemaphoreType.DMA
    scratch = [pltpu.VMEM(tile, bf16)] * 3 + [pltpu.VMEM((zn, own, nar), bf16), pltpu.VMEM(square, bf16)]
    scratch += [pltpu.VMEM((nar, d_all), bf16), pltpu.VMEM(square, bf16), pltpu.VMEM(square, bf16)]
    scratch += [pltpu.VMEM((nar, d_all), bf16), pltpu.VMEM(square, bf16), pltpu.VMEM(square, bf16)]
    scratch += [pltpu.VMEM((own, nar), bf16)]
    scratch += [[dma((h,))] * 4, [dma((zn - 1,))] * 2, [dma((n - 1,))] * 2, [dma((n - 1,))] * 2]
    chunks = 4
    scratch += [[dma((n - 1,))] * 2, [dma((h,))] * 4, [dma((2, zn - 1, chunks))] * 2]
    kernel = functools.partial(chain_kernel, n, zn, chunks, 2.0 / row_count)
    out = (jax.ShapeDtypeStruct((own, d_all), bf16), jax.ShapeDtypeStruct((x.shape[0], own * zn), bf16))
    return call(kernel, out, scratch, 9, 8 * part.nbytes, part, v_pieces, kernel_rows, x)


def front_kernel(n, zn, chunks, g_ref, v_ref, g_out, v_out, send, recv, near, far, mate_send, mate_recv):
    me, z = lax.axis_index("rows"), lax.axis_index("feat")
    core = lax.rem(me, 2)
    mate = me + 1 - 2 * core
    h = n // 2
    own, ck = v_ref.shape[0], g_ref.shape[0] // chunks
    units = chunks + 1
    peers = [lax.rem(me + 2 * d, n) for d in range(1, h)]
    barrier = pltpu.get_barrier_semaphore()
    for target in [mate] + peers:
        pl.semaphore_signal(barrier, inc=1, device_id={"rows": target}, device_id_type=MESH)
    for d in range(1, zn):
        pl.semaphore_signal(barrier, inc=1, device_id={"feat": lax.rem(z + d, zn)}, device_id_type=MESH)
    pl.semaphore_wait(barrier, h + zn - 1)

    def there(block, unit):
        if unit == 0:
            return v_out.at[me, pl.ds(pl.multiple_of(block * own, own), own)]
        return g_out.at[pl.ds((unit - 1) * ck, ck), lanes(block, own)]

    def hop(way, step, unit):
        block = z - step if way == 0 else z + step
        if step == 0:
            src = v_ref if unit == 0 else g_ref.at[pl.ds((unit - 1) * ck, ck)]
        else:
            src = there(block, unit)
        target = lax.rem(z + (1 if way == 0 else zn - 1), zn)
        return remote(src, there(block, unit), send.at[way, step, unit], recv.at[way, step, unit], "feat", target)

    def held(way, step):
        return z >= step if way == 0 else z + step < zn

    def onward(way):
        return z < zn - 1 if way == 0 else z > 0

    def spread(block, d, fresh=False):
        src = v_ref if fresh else there(block, 0)
        return remote(src, there(block, 0), near.at[block, d], far.at[block, d], "rows", peers[d - 1])

    def to_mate(block, d, fresh=False):
        source = lax.rem(me + n - 2 * d, n) if d else me
        ref = v_out.at[source, pl.ds(pl.multiple_of(block * own, own), own)]
        src = v_ref if fresh else ref
        return remote(src, ref, mate_send.at[block, d], mate_recv.at[block, d], "rows", mate)

    def spread_all(block, fresh=False):
        for d in range(1, h):
            spread(block, d, fresh).start()
        to_mate(block, 0, fresh).start()

    def pass_mate(block):
        for d in range(1, h):
            spread(block, d).wait_recv()
            to_mate(block, d).start()

    def each(step, what):
        if step == 0:
            what(z)
            return
        for way in (0, 1):
            @pl.when(held(way, step))
            def _():
                what(z - step if way == 0 else z + step)

    for unit in range(units):
        for way in (0, 1):
            @pl.when(onward(way))
            def _():
                hop(way, 0, unit).start()
    spread_all(z, True)
    v_out[me, pl.ds(pl.multiple_of(z * own, own), own)] = v_ref[...]
    g_out[:, lanes(z, own)] = g_ref[...]
    for step in range(1, zn):
        for unit in range(units):
            for way in (0, 1):
                @pl.when(held(way, step))
                def _():
                    hop(way, step - 1, unit).wait_recv()
                    if step < zn - 1:
                        @pl.when(onward(way))
                        def _():
                            hop(way, step, unit).start()
                    if unit == 0:
                        spread_all(z - step if way == 0 else z + step)
        each(step - 1, pass_mate)
    each(zn - 1, pass_mate)

    def finish(block):
        for d in range(1, h):
            spread(block, d).wait_send()
        for d in range(h):
            to_mate(block, d).wait()

    for step in range(zn):
        each(step, finish)
    for step in range(zn - 1):
        for unit in range(units):
            for way in (0, 1):
                @pl.when(jnp.logical_and(held(way, step), onward(way)))
                def _():
                    hop(way, step, unit).wait_send()


def front(g, v):
    n, zn = lax.axis_size("rows"), lax.axis_size("feat")
    tok, own = g.shape
    chunks = 4
    dma = pltpu.SemaphoreType.DMA
    out = (jax.ShapeDtypeStruct((tok, own * zn), bf16), jax.ShapeDtypeStruct((n, own * zn, v.shape[1]), bf16))
    scratch = [dma((2, zn - 1, chunks + 1))] * 2 + [dma((zn, n // 2))] * 4
    kernel = functools.partial(front_kernel, n, zn, chunks)
    return call(kernel, out, scratch, 10, zn * g.nbytes, g, v)


def divided(lam_row, lam_col, first_row):
    on_diag = (
        (first_row + jnp.arange(lam_row.shape[0], dtype=jnp.int32))[:, None]
        == jnp.arange(lam_col.shape[0], dtype=jnp.int32)[None, :]
    )
    root_row = lam_row ** (-0.5)
    root_col = lam_col ** (-0.5)
    gaps_lam = lam_row[:, None] - lam_col[None, :]
    safe_gap = jnp.where(on_diag, jnp.ones_like(gaps_lam), gaps_lam)
    off_diag = (root_row[:, None] - root_col[None, :]) / safe_gap
    diag_vals = -0.5 * lam_row[:, None] ** (-1.5) + jnp.zeros_like(gaps_lam)
    return jnp.where(on_diag, diag_vals, off_diag)


def dot(a, b, ca, cb):
    return lax.dot_general(a, b, (((ca,), (cb,)), ((), ())), preferred_element_type=f32)


def chain_by_calls(part, v_pieces, kernel_rows, row_count):
    n = lax.axis_size("rows")
    own, d_all = part.shape
    nar = d_all // n
    v_all = v_pieces.transpose(1, 0, 2).reshape(d_all, d_all)
    part = part.reshape(own, n // 2, 2, nar).transpose(2, 1, 0, 3)
    tile = scatter(part, "rows", 3)
    c_col = exchange(tile, "feat", 4, same=True).reshape(n, nar, nar)
    turned = exchange(c_col, "rows", 5)
    both = 0.5 * (c_col.astype(f32) + turned.transpose(0, 2, 1).astype(f32))
    half = dot(v_all, both.reshape(d_all, nar).astype(bf16), 0, 0).astype(bf16)
    half = exchange(half.reshape(n, nar, nar), "rows", 6)
    rotated = dot(half.transpose(1, 0, 2).reshape(nar, d_all), v_all, 1, 0)
    back = dot((kernel_rows * rotated).astype(bf16), v_all, 1, 1).astype(bf16)
    back = exchange(back.reshape(nar, n, nar).transpose(1, 0, 2), "rows", 7).reshape(d_all, nar)
    v_own = lax.dynamic_slice_in_dim(v_all, lax.axis_index("feat") * own, own)
    sens = (2.0 / row_count * dot(v_own, back, 1, 0)).astype(bf16)
    return gather(sens, "rows", 8).transpose(1, 0, 2).reshape(own, d_all)


def local(features, grad_out, eigvecs, eigvals, whiten):
    tok_rows, own = features.shape
    n = lax.axis_size("rows")
    d_all = eigvals.shape[0]
    nar = d_all // n
    row_count = tok_rows * n
    me = lax.axis_index("rows")

    sums = jnp.stack([jnp.sum(features, axis=0, dtype=f32), jnp.sum(grad_out, axis=0, dtype=f32)])
    sums = jnp.pad(sums, ((0, 6), (0, 0)))
    means = jnp.sum(gather(sums, "rows", 1), axis=0) / row_count
    xc = (features.astype(f32) - means[0]).astype(bf16)
    gc = (grad_out.astype(f32) - means[1]).astype(bf16)
    g_all, v_pieces = front(gc, eigvecs.astype(bf16))
    first = me * nar
    lam_row = lax.dynamic_slice_in_dim(eigvals, first, nar)
    kernel_rows = divided(lam_row, eigvals, first)
    part = dot(xc, g_all, 0, 0).astype(bf16)
    if nar % 128 == 0:
        sens, x_all = chain(part, v_pieces, kernel_rows, xc, row_count)
    else:
        x_all = lax.all_gather(xc, "feat", axis=1, tiled=True)
        sens = chain_by_calls(part, v_pieces, kernel_rows, row_count)
    grad_in = dot(g_all, whiten, 1, 0) + dot(x_all, sens, 1, 1)
    return grad_in.astype(bf16)


def solution(mesh):
    in_specs = (P("rows", "feat"), P("rows", "feat"), P("feat", "rows"), P(), P(None, "feat"))
    out_specs = P("rows", "feat")
    return jax.shard_map(local, mesh=mesh, in_specs=in_specs, out_specs=out_specs, check_vma=False)
```

profile of v0, /device:TPU:1, one launch (start us, length us, event | category | flops | bytes accessed | tf_op | source)
XLA Modules:
  0.0 332.8 jit_solution(365352873655480881)
XLA Ops:
  6.5 0.0 copy-start
  6.5 0.0 all-gather.2.cloned.1.call-start
  6.5 1.3 convert_reduce_fusion
  7.8 1.2 convert_reduce_fusion.1
  9.0 0.0 copy-start.2
  9.0 0.0 copy-start.3
  9.1 0.0 copy-start.6
  9.1 12.6 %shard_map.55 = f32[32,8,256]{2,1,0:T(8,128)S(1)} custom-call(f32[8,256]{1,0:T(8,128)S(1)} %select_maximum_fusion.x_ref), custom_call_target="tpu_custom_call" | custom-call | flops 8000000000 | bytes 8192 | tf_op jit(solution)/shard_map/pallas_call | solution.py:108
  21.8 0.0 copy-done.2
  21.8 0.9 fusion.4
  22.7 0.0 all-gather.2.cloned.1.call-update
  22.7 0.0 copy-done.3
  22.7 0.1 fusion.3.g_ref
  22.8 0.0 copy-done.6
  22.8 0.1 copy.20.v_ref
  23.0 0.0 copy-start.4
  23.0 152.9 %shard_map.56 = (bf16[1024,2048]{1,0:T(8,128)(2,1)S(1)}, bf16[32,2048,64]{2,1,0:T(8,128)(2,1)}) custom-call(bf16[1024,256]{1,0:T(8,128)(2,1)S(1)} %fusion.3.g_ref, bf16[256,64]{1,0:T(8,128)(2,1)S(1)} %copy.20.v_ref), custom_call_target="tpu_custom_call" | custom-call | flops 8000000000 | bytes 4194304 | tf_op jit(solution)/shard_map/pallas_call | solution.py:108
  175.9 0.0 copy-start.1
  175.9 1.9 copy-done.1
  177.9 0.0 copy-done.4
  177.9 1.3 convolution_convert_fusion
  179.1 1.3 copy.22
  180.4 2.0 copy.23
  182.5 21.5 %shard_map.57.x_ref = bf16[256,64]{1,0:T(8,128)(2,1)S(1)} custom-call(bf16[2,16,256,64]{3,2,1,0:T(8,128)(2,1)S(1)} %bitcast.36), custom_call_target="tpu_custom_call" | custom-call | flops 8000000000 | bytes 1048576 | tf_op jit(solution)/shard_map/pallas_call | solution.py:108
  204.0 14.0 %shard_map.58 = bf16[8,256,64]{2,1,0:T(8,128)(2,1)S(1)} custom-call(bf16[256,64]{1,0:T(8,128)(2,1)S(1)} %shard_map.57.x_ref), custom_call_target="tpu_custom_call" | custom-call | flops 8000000000 | bytes 32768 | tf_op jit(solution)/shard_map/pallas_call | solution.py:108
  218.0 16.3 %shard_map.59 = bf16[32,64,64]{2,1,0:T(8,128)(2,1)S(1)} custom-call(bf16[32,64,64]{2,1,0:T(8,128)(2,1)S(1)} %bitcast.38), custom_call_target="tpu_custom_call" | custom-call | flops 8000000000 | bytes 262144 | tf_op jit(solution)/shard_map/pallas_call | solution.py:108
  234.3 0.3 copy.24
  234.6 15.9 %copy.21 = bf16[2048,32,64]{0,2,1:T(8,128)(2,1)} copy(bf16[2048,32,64]{2,0,1:T(8,128)(2,1)} %bitcast.47) | data formatting | bytes 16777216 | tf_op jit(solution)/shard_map/transpose | solution.py:495
  250.5 0.2 fusion.6
  250.7 6.0 %convolution_convert_fusion.2 = bf16[2048,64]{0,1:T(8,128)(2,1)S(1)} fusion(bf16[2048,2048]{0,1:T(8,128)(2,1)} %bitcast.44, bf16[2048,64]{1,0:T(8,128)(2,1)S(1)} %bitcast.49), kind=kOutput, calls=%fused_computation.4 | convolution fusion | flops 537001984 | bytes 8912896 | tf_op jit(solution)/shard_map/dot_general | solution.py:488
  256.7 0.3 copy.25
  257.0 0.0 copy-start.7
  257.0 12.9 %shard_map.60 = bf16[32,64,64]{2,1,0:T(8,128)(2,1)S(1)} custom-call(bf16[32,64,64]{2,1,0:T(8,128)(2,1)S(1)} %bitcast.40), custom_call_target="tpu_custom_call" | custom-call | flops 8000000000 | bytes 262144 | tf_op jit(solution)/shard_map/pallas_call | solution.py:108
  269.9 0.3 copy.26
  270.2 0.5 reshape.41
  270.7 0.0 copy-done.7
  270.7 0.1 power_multiply_fusion
  270.8 9.9 %convolution_convert_fusion.1 = bf16[64,2048]{1,0:T(8,128)(2,1)S(1)} fusion(bf16[2048,2048]{0,1:T(8,128)(2,1)} %bitcast.45, bf16[64,2048]{1,0:T(8,128)(2,1)S(1)} %reshape.41, f32[2048]{0:T(1024)S(1)} %copy-done.7, f32[64]{0:T(128)S(1)} %get-tuple-element.10, f32[2048]{0:T(1024)S(1)} %broadcast_power_fusion, f32[64]{0:T(128)S(1)} %broadcast_power_fusion.1, ...), kind=kOutput, calls=%fused_computation.3 | convolution fusion | flops 1074921472 | bytes 8930304 | tf_op jit(solution)/shard_map/dot_general | solution.py:488
  280.7 0.5 reshape.42
  281.3 0.2 copy.33
  281.5 13.1 %shard_map.61 = bf16[32,64,64]{2,1,0:T(8,128)(2,1)S(1)} custom-call(bf16[32,64,64]{2,1,0:T(8,128)(2,1)S(1)} %bitcast.41), custom_call_target="tpu_custom_call" | custom-call | flops 8000000000 | bytes 262144 | tf_op jit(solution)/shard_map/pallas_call | solution.py:108
  294.6 1.7 fusion.2.x_ref
  296.3 20.2 %shard_map.62 = bf16[32,256,64]{2,1,0:T(8,128)(2,1)S(1)} custom-call(bf16[256,64]{1,0:T(8,128)(2,1)S(1)} %fusion.2.x_ref), custom_call_target="tpu_custom_call" | custom-call | flops 8000000000 | bytes 32768 | tf_op jit(solution)/shard_map/pallas_call | solution.py:108
  316.6 1.6 copy.30
  318.2 0.0 copy-done
  318.2 3.5 %fusion.23 = f32[1024,256]{1,0:T(8,128)S(1)} fusion(bf16[1024,2048]{1,0:T(8,128)(2,1)} %copy-done.1, bf16[2048,256]{1,0:T(8,128)(2,1)S(1)} %copy-done), kind=kOutput, calls=%fused_computation.43 | convolution fusion | flops 1073741824 | bytes 6291456 | tf_op jit(solution)/shard_map/dot_general | solution.py:488
  321.7 0.0 all-gather.2.cloned.1.call-done
  321.8 4.2 %fusion.1 = bf16[1024,256]{1,0:T(8,128)(2,1)} fusion(f32[1024,256]{1,0:T(8,128)S(1)} %fusion.23, bf16[1024,2048]{1,0:T(8,128)(2,1)} %all-gather.2.cloned.1.call-done, bf16[256,2048]{0,1:T(8,128)(2,1)S(1)} %bitcast.50), kind=kOutput, calls=%fused_computation.10 | convolution fusion | flops 1074266112 | bytes 6815744 | tf_op jit(solution)/shard_map/dot_general | solution.py:488
  (10 shorter events, 0.1 us)
Async XLA Ops:
  6.5 311.6 %copy-start = (bf16[2048,256]{1,0:T(8,128)(2,1)S(1)}, bf16[2048,256]{1,0:T(8,128)(2,1)}, u32[]{:S(2)}) copy-start(bf16[2048,256]{1,0:T(8,128)(2,1)} %param.9) | copy-start | bytes 3145732
  6.5 315.2 %all-gather.2.cloned.1.call-start = ((), (), s32[]{:S(2)}) async-start(), calls=%async_computation | async-start | bytes 4718592 | tf_op jit(solution)/shard_map/all_gather | solution.py:532
  9.0 12.7 %copy-start.2 = (bf16[1024,256]{1,0:T(8,128)(2,1)S(1)}, bf16[1024,256]{1,0:T(8,128)(2,1)}, u32[]{:S(2)}) copy-start(bf16[1024,256]{1,0:T(8,128)(2,1)} %param.5) | copy-start | bytes 1572868
  9.0 13.7 %copy-start.3 = (bf16[1024,256]{1,0:T(8,128)(2,1)S(1)}, bf16[1024,256]{1,0:T(8,128)(2,1)}, u32[]{:S(2)}) copy-start(bf16[1024,256]{1,0:T(8,128)(2,1)} %param.6) | copy-start | bytes 1572868
  9.1 13.8 %copy-start.6 = (f32[256,64]{0,1:T(8,128)S(1)}, f32[256,64]{0,1:T(8,128)}, u32[]{:S(2)}) copy-start(f32[256,64]{0,1:T(8,128)} %param.7) | copy-start | bytes 196612
  23.0 154.9 %copy-start.4 = (bf16[1024,256]{1,0:T(8,128)(2,1)S(1)}, bf16[1024,256]{1,0:T(8,128)(2,1)}, u32[]{:S(2)}) copy-start(bf16[1024,256]{1,0:T(8,128)(2,1)} %fusion.4) | copy-start | bytes 1572868
  175.9 1.9 copy-start.1
  257.0 13.7 %copy-start.7 = (f32[2048]{0:T(1024)S(1)}, f32[2048]{0:T(1024)}, u32[]{:S(2)}) copy-start(f32[2048]{0:T(1024)} %param.8) | copy-start | bytes 24580
  318.2 3.6 %copy-start.5 = (bf16[256,32,64]{0,2,1:T(8,128)(2,1)S(1)}, bf16[256,32,64]{0,2,1:T(8,128)(2,1)}, u32[]{:S(2)}) copy-start(bf16[256,32,64]{0,2,1:T(8,128)(2,1)} %copy.30) | copy-start | bytes 3145732
Sparse Core Ops, SparseCore 0:
  22.8 105.2 all-gather.1
where the time goes:
time: 333 us
  Pallas kernels  264 us (79%)
  matrix products  26.7 us (8%)
  local copies, waits for them, and re-layouts  25 us (8%)
  between operations  13.7 us (4%)
  other arithmetic  3.82 us (1%)
    pallas_call x8, Pallas kernels, call(): pl.pallas_call(kernel, out_shape=out, in_specs=[VMEM] * len(args), out_sp...  264 us
    dot_general x6, matrix products, dot(): lax.dot_general(a, b, (((ca,), (cb,)), ((), ())), preferred_element_type=...  26.7 us
    transpose x1, local copies, waits for them, and re-layouts, chain_by_calls(): v_all = v_pieces.transpose(1, 0, 2).reshape(d_all, d_all)  15.9 us
  transfers between devices with their start and end apart: 1, of which 0 were waited for; matrix products, arithmetic and copies ran while one was open for 14% of the time, Pallas kernels for 75%

commit v1 on v0

v1 whole, which is shorter than its diff:
```python
import functools
import math

import jax
import jax.numpy as jnp
from jax import lax
from jax.experimental import pallas as pl
from jax.experimental.pallas import tpu as pltpu
from jax.sharding import PartitionSpec as P

MESH = pl.DeviceIdType.MESH
VMEM = pl.BlockSpec(memory_space=pltpu.VMEM)
bf16, f32 = jnp.bfloat16, jnp.float32
CHUNKS = 4


def remote(src, dst, send, recv, axis, target):
    return pltpu.make_async_remote_copy(
        src_ref=src, dst_ref=dst, send_sem=send, recv_sem=recv,
        device_id={axis: target}, device_id_type=MESH,
    )


def lanes(index, width):
    return pl.ds(pl.multiple_of(index * width, width), width)


def mm(a, b, ca=1, cb=0):
    return lax.dot_general(a, b, (((ca,), (cb,)), ((), ())), preferred_element_type=f32)


def slot_order(zn):
    order = [0]
    for dist in range(1, zn // 2):
        order += [zn - dist, dist]
    return order + [zn // 2]


def body(n, zn, row_count, x_ref, g_ref, v_ref, k_ref, w_ref, o_ref,
         x_all, g_all, v_all, v_pair, xct, gc, acc, sums, sums_own, means, pieces, parts, tot, tile, rtile, spiece, sall,
         vct, yacc, yown, yall, mt, town, tall,
         ring_s, ring_r, vr_s, vr_r, vm_s, vm_r, v1_s, v1_r, v2_s, v2_r, vd_s, vd_r, su_s, su_r, me_s, me_r,
         rs_s, rs_r, sy_s, sy_r, ag_s, ag_r, am_s, am_r, ya_s, ya_r):
    me, z = lax.axis_index("rows"), lax.axis_index("feat")
    core, chip = lax.rem(me, 2), me // 2
    mate = me + 1 - 2 * core
    h = n // 2
    nx = math.isqrt(h)
    ny = h // nx
    yy, xx = chip // nx, lax.rem(chip, nx)
    half = zn // 2
    tok, own = x_ref.shape
    nar = k_ref.shape[0]
    wide = 2 * nar
    hv = own // 2
    rp = own // n
    ck = tok // CHUNKS
    order = slot_order(zn)
    every = list(range(CHUNKS))
    pending = []

    barrier = pltpu.get_barrier_semaphore()
    for d in range(1, n):
        pl.semaphore_signal(barrier, inc=1, device_id={"rows": lax.rem(me + d, n)}, device_id_type=MESH)
    for d in range(1, zn):
        pl.semaphore_signal(barrier, inc=1, device_id={"feat": lax.rem(z + d, zn)}, device_id_type=MESH)
    pl.semaphore_wait(barrier, n + zn - 2)

    def at_z(rel):
        return lax.rem(z + rel, zn)

    def block_of(way, dist):
        return at_z(zn - dist) if way == 0 else at_z(dist)

    def next_of(way):
        return at_z(1) if way == 0 else at_z(zn - 1)

    def units(step, way):
        if step < half - 1:
            return every
        return every[: CHUNKS // 2] if way == 0 else every[CHUNKS // 2:]

    def hop(arr, way, step, unit):
        full, mine = (g_all, g_ref) if arr == 0 else (x_all, x_ref)
        there = full.at[block_of(way, step), pl.ds(unit * ck, ck)]
        src = there if step else mine.at[pl.ds(unit * ck, ck)]
        return remote(src, there, ring_s.at[arr, way, step, unit], ring_r.at[arr, way, step, unit], "feat", next_of(way))

    def vpart(block, rows_half, lane, count=1):
        start = pl.multiple_of(block * own + rows_half * hv, hv)
        return v_all.at[pl.ds(start, hv), pl.ds(pl.multiple_of(lane * wide, wide), wide * count)]

    def vhop(way, step):
        ref = vpart(block_of(way, step), core, chip)
        return remote(ref, ref, vr_s.at[way, step], vr_r.at[way, step], "feat", next_of(way))

    def y_first(rel):
        return rel == 0 or rel > half

    def v_one(rel, d):
        ref = vpart(at_z(rel), core, chip)
        if y_first(rel):
            target = (lax.rem(yy + d, ny) * nx + xx) * 2 + core
        else:
            target = (yy * nx + lax.rem(xx + d, nx)) * 2 + core
        return remote(ref, ref, v1_s.at[rel, d - 1], v1_r.at[rel, d - 1], "rows", target)

    def v_two(rel):
        copies = []
        if y_first(rel):
            for e in range(ny):
                ref = vpart(at_z(rel), core, lax.rem(yy + ny - e, ny) * nx + xx)
                for d in range(1, nx):
                    i = e * (nx - 1) + d - 1
                    target = (yy * nx + lax.rem(xx + d, nx)) * 2 + core
                    copies.append(remote(ref, ref, v2_s.at[rel, i], v2_r.at[rel, i], "rows", target))
        else:
            start = pl.multiple_of(at_z(rel) * own + core * hv, hv)
            ref = v_all.at[pl.ds(start, hv), lanes(yy, nx * wide)]
            for d in range(1, ny):
                target = (lax.rem(yy + d, ny) * nx + xx) * 2 + core
                copies.append(remote(ref, ref, v2_s.at[rel, d - 1], v2_r.at[rel, d - 1], "rows", target))
        return copies

    def ones(rel):
        return range(1, ny if y_first(rel) else nx)

    def v_start(rel):
        for d in ones(rel):
            v_one(rel, d).start()

    def v_second(rel):
        for d in ones(rel):
            v_one(rel, d).wait_recv()
        for copy in v_two(rel):
            copy.start()

    def v_mate(rel):
        start = pl.multiple_of(at_z(rel) * own + core * hv, hv)
        ref = v_all.at[pl.ds(start, hv)]
        return remote(ref, ref, vd_s.at[rel], vd_r.at[rel], "rows", mate)

    def v_third(rel):
        for copy in v_two(rel):
            copy.wait_recv()
        v_mate(rel).start()

    for way in (0, 1):
        hop(0, way, 0, units(0, way)[0]).start()
    v_pair[core] = v_ref[...].astype(bf16)
    pair = remote(v_pair.at[core], v_pair.at[core], vm_s.at[0], vm_r.at[0], "rows", mate)
    pair.start()
    sums_own[...] = jnp.zeros_like(sums_own)
    sums_own[0:1] = jnp.sum(x_ref[...].astype(f32), axis=0, keepdims=True)
    sums_own[1:2] = jnp.sum(g_ref[...].astype(f32), axis=0, keepdims=True)
    pair.wait_recv()
    v_all[pl.ds(pl.multiple_of(z * own, own), own), lanes(chip, wide)] = jnp.concatenate([v_pair[0], v_pair[1]], axis=1)
    for way in (0, 1):
        if way == 0 or half > 1:
            vhop(way, 0).start()
        for unit in units(0, way)[1:]:
            hop(0, way, 0, unit).start()
    sum_copies = []
    for d in range(1, n):
        copy = remote(sums_own, sums.at[me], su_s.at[d - 1], su_r.at[d - 1], "rows", lax.rem(me + d, n))
        copy.start()
        sum_copies.append(copy)
    sums[me] = sums_own[...]
    pending += sum_copies + [pair]
    v_start(0)
    x_all[z] = x_ref[...]
    for copy in sum_copies:
        copy.wait_recv()
    means[z] = jnp.sum(sums[...], axis=0) / row_count
    mean_copies = []
    for d in range(1, zn):
        copy = remote(means.at[z], means.at[z], me_s.at[d - 1], me_r.at[d - 1], "feat", at_z(d))
        copy.start()
        mean_copies.append(copy)
    pending += mean_copies
    xc = (x_ref[...].astype(f32) - means[z, 0:1]).astype(bf16)
    xct[...] = xc.astype(f32).T.astype(bf16)

    def gram(slot):
        rel = order[slot]
        q = at_z(rel)
        src = g_ref if rel == 0 else g_all.at[q]
        gc[...] = (src[...].astype(f32) - means[q, 1:2]).astype(bf16)
        block = mm(xct[...], gc[...])
        lane = pl.ds(slot * own, own)

        def put(value):
            pieces[:, :, lane] = value.reshape(n, rp, own).astype(bf16)

        if rel == 0:
            put(0.5 * (block + block.T))
        else:
            @pl.when(z < q)
            def _():
                put(0.5 * block)

            @pl.when(z > q)
            def _():
                put(0.5 * block.T)
        gw = mm(gc[...], w_ref[pl.ds(pl.multiple_of(q * own, own), own)])
        acc[...] = gw if slot == 0 else acc[...] + gw

    split = max(1, zn - 3)
    groups = [(0, split), (split, zn)]

    def rs(group, d):
        lo, hi = groups[group]
        lane = pl.ds(lo * own, (hi - lo) * own)
        s = lax.rem(me + d, n)
        return remote(pieces.at[s, :, lane], parts.at[me, :, lane], rs_s.at[group, d - 1], rs_r.at[group, d - 1], "rows", s)

    def rs_start(group):
        for d in range(1, n):
            rs(group, d).start()

    def rs_sum(group):
        lo, hi = groups[group]
        lane = pl.ds(lo * own, (hi - lo) * own)
        total = pieces[me, :, lane].astype(f32)
        for d in range(1, n):
            rs(group, d).wait_recv()
            total = total + parts[lax.rem(me + n - d, n), :, lane].astype(f32)
        for slot in range(lo, hi):
            tile[slot] = total[:, (slot - lo) * own:(slot - lo + 1) * own].astype(bf16)

    gram(0)
    rels = [[0]]
    started = False
    first_wait = True
    for dist in range(1, half + 1):
        got = []
        for way in (0, 1):
            if way == 0 or dist < half:
                vhop(way, dist - 1).wait_recv()
                if (way == 0 and dist < half) or (way == 1 and dist < half - 1):
                    vhop(way, dist).start()
                rel = zn - dist if way == 0 else dist
                v_start(rel)
                got.append(rel)
        rels.append(got)
        if dist == half and zn > 2:
            pass
        for unit in every:
            for way in (0, 1):
                if unit in units(dist - 1, way):
                    hop(0, way, dist - 1, unit).wait_recv()
                    if dist < half and unit in units(dist, way):
                        hop(0, way, dist, unit).start()
        if dist == half - 1 or half == 1:
            for unit in every:
                for way in (0, 1):
                    if unit in units(0, way):
                        hop(1, way, 0, unit).start()
        for rel in rels[dist - 1]:
            v_second(rel)
        if dist >= 2:
            for rel in rels[dist - 2]:
                v_third(rel)
        if first_wait:
            for copy in mean_copies:
                copy.wait_recv()
            first_wait = False
        for slot in range(zn):
            if order[slot] in (dist, zn - dist):
                gram(slot)
                if slot == split - 1:
                    rs_start(0)
        if split == 1 and dist == 1:
            rs_start(0)
    rs_start(1)
    for rel in rels[half]:
        v_second(rel)
    for rel in rels[half - 1]:
        v_third(rel)

    forwards = [(step, unit) for step in range(1, half) for unit in every]
    state = {"next": 0}

    def pump(count):
        for _ in range(count):
            if state["next"] < len(forwards):
                step, unit = forwards[state["next"]]
                state["next"] += 1
                for way in (0, 1):
                    if unit in units(step - 1, way):
                        hop(1, way, step - 1, unit).wait_recv()
                        if unit in units(step, way):
                            hop(1, way, step, unit).start()

    rs_sum(0)
    rs_sum(1)

    sym = []
    for slot in range(1, zn):
        d = order[slot]
        copy = remote(tile.at[slot], rtile.at[order.index((zn - d) % zn)], sy_s.at[d - 1], sy_r.at[d - 1], "feat", at_z(d))
        copy.start()
        sym.append(copy)
    pending += sym
    for rel in rels[half]:
        v_third(rel)
    pump(2)
    for copy in sym:
        copy.wait_recv()
    spiece[:, pl.ds(0, own)] = tile[0]
    for slot in range(1, zn):
        both = tile[slot].astype(f32) + rtile[slot].astype(f32)
        spiece[:, pl.ds(slot * own, own)] = both.astype(bf16)

    def gather_start(which, src, full):
        copies = []
        for d in range(1, h):
            copy = remote(src, full.at[me], ag_s.at[which, d], ag_r.at[which, d], "rows", lax.rem(me + 2 * d, n))
            copy.start()
            copies.append(copy)
        passed = remote(src, full.at[me], am_s.at[which, 0], am_r.at[which, 0], "rows", mate)
        passed.start()
        full[me] = src[...]
        return copies, [passed]

    def gather_end(which, full, copies, passed):
        for d in range(1, h):
            source = lax.rem(me + n - 2 * d, n)
            copies[d - 1].wait_recv()
            copy = remote(full.at[source], full.at[source], am_s.at[which, d], am_r.at[which, d], "rows", mate)
            copy.start()
            passed.append(copy)
        for copy in passed:
            copy.wait_recv()
        return copies + passed

    copies, passed = gather_start(0, spiece, sall)
    for rel in range(zn):
        v_mate(rel).wait_recv()
    vct[...] = v_all[:, lanes(chip, wide)].astype(f32).T.astype(bf16)
    pump(2)
    pending += gather_end(0, sall, copies, passed)

    yacc[...] = jnp.zeros_like(yacc)
    own_rows = pl.ds(pl.multiple_of(core * nar, nar), nar)
    for slot in range(zn):
        q = at_z(order[slot])
        block = sall[:, :, pl.ds(slot * own, own)].astype(f32).reshape(own, own).astype(bf16)
        left = vct[own_rows, lanes(q, own)]
        if slot == 0:
            yacc[...] += mm(left, block)
        else:
            @pl.when(q < z)
            def _():
                yacc[...] += mm(left, block)

            @pl.when(q > z)
            def _():
                yacc[...] += mm(left, block, 1, 1)
    yown[...] = yacc[...].astype(bf16)
    ysend = []
    for d in range(1, zn):
        copy = remote(yown, yall.at[z], ya_s.at[d - 1], ya_r.at[d - 1], "feat", at_z(d))
        copy.start()
        ysend.append(copy)
    pending += ysend
    yall[z] = yown[...]
    pump(2)
    for copy in ysend:
        copy.wait_recv()
    d_all = v_all.shape[0]
    left = jnp.concatenate([yall[q] for q in range(zn)], axis=1)
    mt[...] = (k_ref[...] * mm(left, v_all[...])).astype(bf16)
    town[...] = mm(mt[...], v_all[pl.ds(pl.multiple_of(z * own, own), own)], 1, 1).astype(bf16)
    copies, passed = gather_start(1, town, tall)
    pump(len(forwards))
    pending += gather_end(1, tall, copies, passed)
    for way in (0, 1):
        for unit in units(half - 1, way):
            hop(1, way, half - 1, unit).wait_recv()

    @pl.loop(0, zn)
    def _(q):
        sens = mm(v_all[pl.ds(pl.multiple_of(q * own, own), own)], tall[...].reshape(d_all, own))
        sens = ((2.0 / row_count) * sens).astype(bf16)
        xq = (x_all[q].astype(f32) - means[q, 0:1]).astype(bf16)
        acc[...] += mm(xq, sens)

    o_ref[...] = acc[...].astype(bf16)

    for copy in pending:
        copy.wait_send()
    for group in range(2):
        for d in range(1, n):
            rs(group, d).wait_send()
    for arr in (0, 1):
        for way in (0, 1):
            for step in range(half):
                for unit in units(step, way):
                    hop(arr, way, step, unit).wait_send()
    for step in range(half):
        for way in (0, 1):
            if way == 0 or step < half - 1:
                vhop(way, step).wait_send()
    for rel in range(zn):
        for d in ones(rel):
            v_one(rel, d).wait_send()
        for copy in v_two(rel):
            copy.wait_send()
        v_mate(rel).wait_send()


def divided(lam_row, lam_col, first_row):
    on_diag = (
        (first_row + jnp.arange(lam_row.shape[0], dtype=jnp.int32))[:, None]
        == jnp.arange(lam_col.shape[0], dtype=jnp.int32)[None, :]
    )
    root_row = lam_row ** (-0.5)
    root_col = lam_col ** (-0.5)
    gaps_lam = lam_row[:, None] - lam_col[None, :]
    safe_gap = jnp.where(on_diag, jnp.ones_like(gaps_lam), gaps_lam)
    off_diag = (root_row[:, None] - root_col[None, :]) / safe_gap
    diag_vals = -0.5 * lam_row[:, None] ** (-1.5) + jnp.zeros_like(gaps_lam)
    return jnp.where(on_diag, diag_vals, off_diag)


def local(features, grad_out, eigvecs, eigvals, whiten):
    tok, own = features.shape
    n, zn = lax.axis_size("rows"), lax.axis_size("feat")
    d_all = eigvals.shape[0]
    nar, rp = d_all // n, own // n
    h, half = n // 2, zn // 2
    nx = math.isqrt(h)
    row_count = tok * n
    first = lax.axis_index("rows") * nar
    kernel_rows = divided(lax.dynamic_slice_in_dim(eigvals, first, nar), eigvals, first)
    scratch = [
        pltpu.VMEM((zn, tok, own), bf16),
        pltpu.VMEM((zn, tok, own), bf16),
        pltpu.VMEM((d_all, d_all), bf16),
        pltpu.VMEM((2, own, nar), bf16),
        pltpu.VMEM((own, tok), bf16),
        pltpu.VMEM((tok, own), bf16),
        pltpu.VMEM((tok, own), f32),
        pltpu.VMEM((n, 8, own), f32),
        pltpu.VMEM((8, own), f32),
        pltpu.VMEM((zn, 8, own), f32),
        pltpu.VMEM((n, rp, d_all), bf16),
        pltpu.VMEM((n, rp, d_all), bf16),
        pltpu.VMEM((8, 128), f32),
        pltpu.VMEM((zn, rp, own), bf16),
        pltpu.VMEM((zn, rp, own), bf16),
        pltpu.VMEM((rp, d_all), bf16),
        pltpu.VMEM((n, rp, d_all), bf16),
        pltpu.VMEM((2 * nar, d_all), bf16),
        pltpu.VMEM((nar, own), f32),
        pltpu.VMEM((nar, own), bf16),
        pltpu.VMEM((zn, nar, own), bf16),
        pltpu.VMEM((nar, d_all), bf16),
        pltpu.VMEM((nar, own), bf16),
        pltpu.VMEM((n, nar, own), bf16),
    ]

    def sems(*shape):
        return [pltpu.SemaphoreType.DMA(shape)] * 2

    scratch += sems(2, 2, half, CHUNKS) + sems(2, half) + sems(1) + sems(zn, nx) + sems(zn, nx * nx) + sems(zn)
    scratch += sems(n - 1) + sems(zn - 1) + sems(2, n - 1) + sems(zn - 1) + sems(2, h) + sems(2, h) + sems(zn - 1)
    return pl.pallas_call(
        functools.partial(body, n, zn, row_count),
        out_shape=jax.ShapeDtypeStruct((tok, own), bf16),
        in_specs=[VMEM] * 5,
        out_specs=VMEM,
        scratch_shapes=scratch,
        compiler_params=pltpu.CompilerParams(collective_id=1, has_side_effects=True, vmem_limit_bytes=58 * 2**20),
        cost_estimate=pl.CostEstimate(flops=8_000_000_000, bytes_accessed=16 * 2**20, transcendentals=0),
    )(features, grad_out, eigvecs, kernel_rows, whiten)


def solution(mesh):
    in_specs = (P("rows", "feat"), P("rows", "feat"), P("feat", "rows"), P(), P(None, "feat"))
    out_specs = P("rows", "feat")
    return jax.shard_map(local, mesh=mesh, in_specs=in_specs, out_specs=out_specs, check_vma=False)
```

time: 333 us -> 135 us (0.41)
  Pallas kernels: 264 us -> 130 us
  matrix products: 26.7 us -> 0 us
  local copies, waits for them, and re-layouts: 25 us -> 4.17 us
  between operations: 13.7 us -> 0.02 us
    pallas_call x8 -> x1, Pallas kernels: 264 us -> 130 us  [local(): pl.pallas_call(functools.partial(body, n, zn, row_count), out_shape=jax.S...]
    dot_general x6 -> x0, matrix products: 26.7 us -> none  [dot(): lax.dot_general(a, b, (((ca,), (cb,)), ((), ())), preferred_element_type=...]
    transpose x3 -> x0, local copies, waits for them, and re-layouts: 17.8 us -> none  [the longest x1 15.9 us: chain_by_calls(): v_all = v_pieces.transpose(1, 0, 2).reshape(d_all, d_all)]
  transfers between devices with their start and end apart: 1 -> 0, of which waited for: 0 -> 0; matrix products, arithmetic and copies ran while one was open for 14% -> 0% of each run, Pallas kernels for 75% -> 0%
where the time goes in v1:
time: 135 us
  Pallas kernels  130 us (96%)
  local copies, waits for them, and re-layouts  4.17 us (3%)
    pallas_call x1, Pallas kernels, local(): pl.pallas_call(functools.partial(body, n, zn, row_count), out_shape=jax.S...  130 us
    unnamed x4, local copies, waits for them, and re-layouts  4.15 us

profile of v1, /device:TPU:1, one launch (start us, length us, event | category | flops | bytes accessed | tf_op | source)
XLA Modules:
  0.0 135.1 jit_solution(10315959932522153267)
XLA Ops:
  0.0 0.0 copy-start
  0.0 0.7 copy-done
  0.7 0.1 power_multiply_fusion
  0.8 1.6 %copy.6.v_ref = f32[256,64]{1,0:T(8,128)} copy(f32[256,64]{0,1:T(8,128)} %param.7) | data formatting | bytes 131072 | tf_op args[2]
  2.4 1.1 divide_select_fusion.k_ref
  3.4 129.7 %shard_map.55 = bf16[1024,256]{1,0:T(8,128)(2,1)} custom-call(bf16[1024,256]{1,0:T(8,128)(2,1)} %x_ref.1, bf16[1024,256]{1,0:T(8,128)(2,1)} %g_ref.1, f32[256,64]{1,0:T(8,128)} %copy.6.v_ref, f32[64,2048]{1,0:T(8,128)} %divide_select_fusion.k_ref, bf16[2048,256]{1,0:T(8,128)(2,1)} %w_ref.1), custom_call_target="tpu_custom_call" | custom-call | flops 8000000000 | bytes 16777216 | tf_op jit(solution)/shard_map/pallas_call | solution.py:469
  133.2 1.9 %copy.8 = bf16[1024,256]{1,0:T(8,128)(2,1)} copy(bf16[1024,256]{1,0:T(8,128)(2,1)} %shard_map.55) | data formatting | bytes 1048576
  (3 shorter events, 0.0 us)
Async XLA Ops:
  0.0 0.7 copy-start

commit v2 on v1

v2 whole, which is shorter than its diff:
```python
import functools
import math

import jax
import jax.numpy as jnp
from jax import lax
from jax.experimental import pallas as pl
from jax.experimental.pallas import tpu as pltpu
from jax.sharding import PartitionSpec as P

MESH = pl.DeviceIdType.MESH
VMEM = pl.BlockSpec(memory_space=pltpu.VMEM)
bf16, f32 = jnp.bfloat16, jnp.float32
CHUNKS = 4


def remote(src, dst, send, recv, axis, target):
    return pltpu.make_async_remote_copy(
        src_ref=src, dst_ref=dst, send_sem=send, recv_sem=recv,
        device_id={axis: target}, device_id_type=MESH,
    )


def lanes(index, width):
    return pl.ds(pl.multiple_of(index * width, width), width)


def mm(a, b, ca=1, cb=0):
    return lax.dot_general(a, b, (((ca,), (cb,)), ((), ())), preferred_element_type=f32)


def slot_order(zn):
    order = [0]
    for dist in range(1, zn // 2):
        order += [zn - dist, dist]
    return order + [zn // 2]


def body(n, zn, row_count, x_hbm, g_hbm, v_hbm, e_hbm, w_hbm, o_ref,
         x_ref, g_ref, v_ref, e_ref, w_ref, x_all, xc_all, g_all, v_all, v_pair, xct, gc, acc, sums, sums_own, means,
         pieces, parts, tile, rtile, spiece, sall, vct, yacc, yown, yall, kern, mt, town, tall, sens,
         ld, ring_s, ring_r, vr_s, vr_r, vm, v1_s, v1_r, v2_s, v2_r, vd, su, me_sem, rs_sem, sy_sem, ag_sem, am_sem, ya_sem):
    me, z = lax.axis_index("rows"), lax.axis_index("feat")
    core, chip = lax.rem(me, 2), me // 2
    mate = me + 1 - 2 * core
    h = n // 2
    nx = math.isqrt(h)
    ny = h // nx
    yy, xx = chip // nx, lax.rem(chip, nx)
    half = zn // 2
    tok, own = x_ref.shape
    d_all = v_all.shape[0]
    nar = d_all // n
    wide = 2 * nar
    hv = own // 2
    rp = own // n
    ck = tok // CHUNKS
    order = slot_order(zn)
    every = list(range(CHUNKS))
    loads = []
    for i, (src, dst) in enumerate([(g_hbm, g_ref), (v_hbm, v_ref), (x_hbm, x_ref), (e_hbm, e_ref), (w_hbm, w_ref)]):
        load = pltpu.make_async_copy(src, dst, ld.at[i])
        load.start()
        loads.append(load)
    barrier = pltpu.get_barrier_semaphore()
    for d in range(1, n):
        pl.semaphore_signal(barrier, inc=1, device_id={"rows": lax.rem(me + d, n)}, device_id_type=MESH)
    for d in range(1, zn):
        pl.semaphore_signal(barrier, inc=1, device_id={"feat": lax.rem(z + d, zn)}, device_id_type=MESH)
    loads[0].wait()
    loads[1].wait()
    v_pair[core] = v_ref[...].astype(bf16)
    pl.semaphore_wait(barrier, n + zn - 2)

    def at_z(rel):
        return lax.rem(z + rel, zn)

    def rows_of(block, count):
        return pl.ds(pl.multiple_of(block * count, count), count)

    def arrived(ref, sem):
        pltpu.make_async_copy(ref, ref, sem).wait()

    def block_of(way, dist):
        return at_z(zn - dist) if way == 0 else at_z(dist)

    def next_of(way):
        return at_z(1) if way == 0 else at_z(zn - 1)

    def units(step, way):
        if step < half - 1:
            return every
        return every[: CHUNKS // 2] if way == 0 else every[CHUNKS // 2:]

    def hop(arr, way, step, unit):
        full, mine = (g_all, g_ref) if arr == 0 else (x_all, x_ref)
        there = full.at[block_of(way, step), pl.ds(unit * ck, ck)]
        src = there if step else mine.at[pl.ds(unit * ck, ck)]
        return remote(src, there, ring_s.at[arr], ring_r.at[arr, way, step, unit], "feat", next_of(way))

    def vpart(block, lane):
        return v_all.at[rows_of(2 * block + core, hv), lanes(lane, wide)]

    def v_arrived(count, sem):
        if count * wide > d_all:
            arrived(v_all.at[pl.ds(0, count * wide * hv // d_all)], sem)
        elif count:
            arrived(v_all.at[pl.ds(0, hv), pl.ds(0, count * wide)], sem)

    def vhop(way, step):
        ref = vpart(block_of(way, step), chip)
        return remote(ref, ref, vr_s.at[0], vr_r.at[way, step], "feat", next_of(way))

    def y_first(rel):
        return rel == 0 or rel > half

    def by_y(d):
        return (lax.rem(yy + d, ny) * nx + xx) * 2 + core

    def by_x(d):
        return (yy * nx + lax.rem(xx + d, nx)) * 2 + core

    def v_first(rel):
        ref = vpart(at_z(rel), chip)
        for d in range(1, ny if y_first(rel) else nx):
            target = by_y(d) if y_first(rel) else by_x(d)
            remote(ref, ref, v1_s.at[0], v1_r.at[rel], "rows", target).start()

    def v_second(rel):
        v_arrived((ny if y_first(rel) else nx) - 1, v1_r.at[rel])
        if y_first(rel):
            for e in range(ny):
                ref = vpart(at_z(rel), lax.rem(yy + ny - e, ny) * nx + xx)
                for d in range(1, nx):
                    remote(ref, ref, v2_s.at[0], v2_r.at[rel], "rows", by_x(d)).start()
        else:
            ref = v_all.at[rows_of(2 * at_z(rel) + core, hv), lanes(yy, nx * wide)]
            for d in range(1, ny):
                remote(ref, ref, v2_s.at[0], v2_r.at[rel], "rows", by_y(d)).start()

    def v_third(rel):
        v_arrived(ny * (nx - 1) if y_first(rel) else nx * (ny - 1), v2_r.at[rel])
        ref = v_all.at[rows_of(2 * at_z(rel) + core, hv)]
        remote(ref, ref, vd.at[0], vd.at[1], "rows", mate).start()
    for way in (0, 1):
        hop(0, way, 0, units(0, way)[0]).start()
    pair = remote(v_pair.at[core], v_pair.at[core], vm.at[0], vm.at[1], "rows", mate)
    pair.start()
    loads[2].wait()
    sums_own[...] = jnp.zeros_like(sums_own)
    sums_own[0:1] = jnp.sum(x_ref[...].astype(f32), axis=0, keepdims=True)
    sums_own[1:2] = jnp.sum(g_ref[...].astype(f32), axis=0, keepdims=True)
    pair.wait_recv()
    both = jnp.concatenate([v_pair[0].astype(f32), v_pair[1].astype(f32)], axis=0)
    v_all[rows_of(z, own), lanes(chip, wide)] = both.T.astype(bf16)
    for way in (0, 1):
        if way == 0 or half > 1:
            vhop(way, 0).start()
        for unit in units(0, way)[1:]:
            hop(0, way, 0, unit).start()
    for d in range(1, n):
        remote(sums_own, sums.at[me], su.at[0], su.at[1], "rows", lax.rem(me + d, n)).start()
    sums[me] = sums_own[...]
    v_first(0)
    loads[3].wait()
    root = jnp.sqrt(e_ref[...])
    shape = (nar, d_all)
    wanted = me * nar + lax.broadcasted_iota(jnp.int32, shape, 0)
    hit = wanted == lax.broadcasted_iota(jnp.int32, shape, 1)
    root_row = jnp.sum(jnp.where(hit, jnp.broadcast_to(root, shape), 0.0), axis=1, keepdims=True)
    kern[...] = -1.0 / ((root_row * root) * (root_row + root))
    arrived(sums.at[pl.ds(0, n - 1)], su.at[1])
    means[z] = jnp.sum(sums[...], axis=0) / row_count
    for d in range(1, zn):
        remote(means.at[z], means.at[z], me_sem.at[0], me_sem.at[1], "feat", at_z(d)).start()
    xc = x_ref[...].astype(f32) - means[z, 0:1]
    xc_all[z] = xc.astype(bf16)
    xct[...] = xc.T.astype(bf16)
    loads[4].wait()

    def gram(slot):
        rel = order[slot]
        q = at_z(rel)
        src = g_ref if rel == 0 else g_all.at[q]
        gc[...] = (src[...].astype(f32) - means[q, 1:2]).astype(bf16)
        block = mm(xct[...], gc[...])
        lane = pl.ds(slot * own, own)

        def put(value):
            pieces[:, :, lane] = value.reshape(n, rp, own).astype(bf16)

        if rel == 0:
            put(0.5 * (block + block.T))
        else:
            @pl.when(z < q)
            def _():
                put(0.5 * block)

            @pl.when(z > q)
            def _():
                put(0.5 * block.T)

    def product(slot):
        gw = mm(gc[...], w_ref[rows_of(at_z(order[slot]), own)])
        acc[...] = gw if slot == 0 else acc[...] + gw

    split = max(1, zn - 3)
    groups = [(0, split), (split, zn)]
    group_lanes = [pl.ds(lo * own, (hi - lo) * own) for lo, hi in groups]

    def rs_start(group):
        lane = group_lanes[group]
        for d in range(1, n):
            s = lax.rem(me + d, n)
            remote(pieces.at[s, :, lane], parts.at[me, :, lane], rs_sem.at[0, group], rs_sem.at[1, group], "rows", s).start()

    def rs_sum(group):
        (lo, hi), lane = groups[group], group_lanes[group]
        arrived(parts.at[pl.ds(0, n - 1), :, lane], rs_sem.at[1, group])
        total = pieces[me, :, lane].astype(f32)
        for d in range(1, n):
            total = total + parts[lax.rem(me + n - d, n), :, lane].astype(f32)
        for slot in range(lo, hi):
            tile[slot] = total[:, (slot - lo) * own:(slot - lo + 1) * own].astype(bf16)

    def sym_slots(group):
        return range(max(1, groups[group][0]), groups[group][1])

    def sym_start(group):
        for slot in sym_slots(group):
            d = order[slot]
            there = rtile.at[order.index((zn - d) % zn)]
            remote(tile.at[slot], there, sy_sem.at[0, group], sy_sem.at[1, group], "feat", at_z(d)).start()

    def sym_bytes(group):
        return rtile.at[pl.ds(sym_slots(group)[0], len(sym_slots(group)))]

    def sym_end(group):
        if len(sym_slots(group)):
            arrived(sym_bytes(group), sy_sem.at[1, group])
        lo, hi = groups[group]
        for slot in range(lo, hi):
            both = tile[slot].astype(f32)
            if slot:
                both = both + rtile[slot].astype(f32)
            spiece[:, pl.ds(slot * own, own)] = both.astype(bf16)

    def gather_start(which, src, view):
        for d in range(1, h):
            there = lax.rem(chip + d, h)
            remote(src, view(chip, core), ag_sem.at[0, which], ag_sem.at[1, which], "rows", 2 * there + core).start()

    def gather_pass(which, view):
        arrived(view(pl.ds(0, h - 1), core), ag_sem.at[1, which])
        mine = view(pl.ds(0, h), core)
        copy = remote(mine, mine, am_sem.at[0, which], am_sem.at[1, which], "rows", mate)
        copy.start()
        return copy

    def s_view(group):
        return lambda chips, side: sall.at[chips, side, :, group_lanes[group]]

    def t_view(chips, side):
        return tall.at[chips, side]

    done = set()

    def take(arr, way, step, unit):
        if (arr, way, step, unit) not in done:
            done.add((arr, way, step, unit))
            hop(arr, way, step, unit).wait_recv()

    forwards = [(step, unit) for step in range(1, half) for unit in every]
    state = {"next": 0}

    def pump(count):
        for _ in range(count):
            if state["next"] < len(forwards):
                step, unit = forwards[state["next"]]
                state["next"] += 1
                for way in (0, 1):
                    if unit in units(step, way):
                        take(1, way, step - 1, unit)
                        hop(1, way, step, unit).start()

    def all_in(arr, dist):
        for unit in every:
            for way in (0, 1):
                if unit in units(dist - 1, way):
                    take(arr, way, dist - 1, unit)

    def center(rel):
        q = at_z(rel)
        xc_all[q] = (x_all[q].astype(f32) - means[q, 0:1]).astype(bf16)
    gram(0)
    product(0)
    v_second(0)
    rels = [[0]]
    for dist in range(1, half + 1):
        got = []
        for way in (0, 1):
            if way == 0 or dist < half:
                vhop(way, dist - 1).wait_recv()
                if (way == 0 and dist < half) or (way == 1 and dist < half - 1):
                    vhop(way, dist).start()
                rel = zn - dist if way == 0 else dist
                v_first(rel)
                got.append(rel)
        rels.append(got)
        for unit in every:
            for way in (0, 1):
                if unit in units(dist - 1, way):
                    take(0, way, dist - 1, unit)
                    if dist < half and unit in units(dist, way):
                        hop(0, way, dist, unit).start()
            if dist < half and unit == 1:
                for rel in rels[dist - 1]:
                    v_third(rel)
            if dist < half and unit == 2:
                for rel in rels[dist]:
                    v_second(rel)
        if dist == half - 1 or half == 1:
            for unit in every:
                for way in (0, 1):
                    if unit in units(0, way):
                        hop(1, way, 0, unit).start()
        if dist == 1:
            arrived(means.at[pl.ds(0, zn - 1)], me_sem.at[1])
        mine = [slot for slot in range(zn) if order[slot] in (dist, zn - dist)]
        if dist == 1 and split == 1:
            rs_start(0)
        for slot in mine:
            gram(slot)
            if dist < half:
                product(slot)
            if slot == split - 1:
                rs_start(0)
        if dist == half - 1:
            rs_sum(0)
            sym_start(0)
    rs_start(1)
    product(zn - 1)
    if half == 1:
        rs_sum(0)
        sym_start(0)
    sym_end(0)
    sall[chip, core, :, group_lanes[0]] = spiece[:, group_lanes[0]]
    gather_start(0, spiece.at[:, group_lanes[0]], s_view(0))
    if half > 1:
        for rel in rels[half - 1]:
            v_third(rel)
    else:
        v_third(0)
    pump(1)
    for rel in rels[half]:
        v_second(rel)
    rs_sum(1)
    sym_start(1)
    pump(2)
    passes = [gather_pass(0, s_view(0))]
    for rel in rels[half]:
        v_third(rel)
    pump(1)
    sym_end(1)
    sall[chip, core, :, group_lanes[1]] = spiece[:, group_lanes[1]]
    gather_start(1, spiece.at[:, group_lanes[1]], s_view(1))
    arrived(v_all.at[pl.ds(0, d_all // 2)], vd.at[1])
    vct[...] = v_all[:, lanes(chip, wide)].astype(f32).T.astype(bf16)
    yacc[...] = jnp.zeros_like(yacc)

    def y_part(group):
        passes[group].wait_recv()
        lo, hi = groups[group]
        for slot in range(lo, hi):
            q = at_z(order[slot])
            block = sall[:, :, :, pl.ds(slot * own, own)].astype(f32).reshape(own, own).astype(bf16)
            left = vct[rows_of(core, nar), lanes(q, own)]
            if slot == 0:
                yacc[...] += mm(left, block)
            else:
                @pl.when(q < z)
                def _():
                    yacc[...] += mm(left, block)

                @pl.when(q > z)
                def _():
                    yacc[...] += mm(left, block, 1, 1)

    y_part(0)
    pump(2)
    passes.append(gather_pass(1, s_view(1)))
    y_part(1)
    yown[...] = yacc[...].astype(bf16)
    for d in range(1, zn):
        remote(yown, yall.at[z], ya_sem.at[0], ya_sem.at[1], "feat", at_z(d)).start()
    yall[z] = yown[...]
    pump(2)
    if half > 1:
        all_in(1, 1)
        center(zn - 1)
        center(1)
    arrived(yall.at[pl.ds(0, zn - 1)], ya_sem.at[1])
    left = jnp.concatenate([yall[q] for q in range(zn)], axis=1)
    mt[...] = (kern[...] * mm(left, v_all[...])).astype(bf16)
    town[...] = mm(mt[...], v_all[rows_of(z, own)], 1, 1).astype(bf16)
    tall[chip, core] = town[...]
    gather_start(2, town, t_view)
    pump(len(forwards))
    if half > 2:
        all_in(1, 2)
        center(zn - 2)
        center(2)
    passes.append(gather_pass(2, t_view))
    passes[2].wait_recv()
    @pl.loop(0, zn)
    def _(q):
        part = mm(v_all[rows_of(q, own)], tall[...].reshape(d_all, own))
        sens[rows_of(q, own)] = ((2.0 / row_count) * part).astype(bf16)

    def finish(rel):
        q = at_z(rel)
        acc[...] += mm(xc_all[q], sens[rows_of(q, own)])
    finish(0)
    for dist in range(1, half):
        if dist > 2:
            all_in(1, dist)
            center(zn - dist)
            center(dist)
        finish(zn - dist)
        finish(dist)
    all_in(1, half)
    center(half)
    q = at_z(half)
    o_ref[...] = (acc[...] + mm(xc_all[q], sens[rows_of(q, own)])).astype(bf16)
    pair.wait_send()
    for arr, full in ((0, g_all), (1, x_all)):
        arrived(full.at[pl.ds(0, zn - 1)], ring_s.at[arr])
    v_arrived(zn - 1, vr_s.at[0])
    v_arrived(sum((ny if y_first(rel) else nx) - 1 for rel in range(zn)), v1_s.at[0])
    v_arrived(sum(ny * (nx - 1) if y_first(rel) else nx * (ny - 1) for rel in range(zn)), v2_s.at[0])
    arrived(v_all.at[pl.ds(0, d_all // 2)], vd.at[0])
    arrived(sums.at[pl.ds(0, n - 1)], su.at[0])
    arrived(means.at[pl.ds(0, zn - 1)], me_sem.at[0])
    for group in range(2):
        arrived(parts.at[pl.ds(0, n - 1), :, group_lanes[group]], rs_sem.at[0, group])
        if len(sym_slots(group)):
            arrived(sym_bytes(group), sy_sem.at[0, group])
        arrived(s_view(group)(pl.ds(0, h - 1), core), ag_sem.at[0, group])
    arrived(t_view(pl.ds(0, h - 1), core), ag_sem.at[0, 2])
    for copy in passes:
        copy.wait_send()
    arrived(yall.at[pl.ds(0, zn - 1)], ya_sem.at[0])


def local(features, grad_out, eigvecs, eigvals, whiten):
    tok, own = features.shape
    n, zn = lax.axis_size("rows"), lax.axis_size("feat")
    d_all = eigvals.shape[0]
    nar, rp = d_all // n, own // n
    h, half = n // 2, zn // 2
    row_count = tok * n
    scratch = [
        pltpu.VMEM((tok, own), bf16),
        pltpu.VMEM((tok, own), bf16),
        pltpu.VMEM((nar, own), f32),
        pltpu.VMEM((1, d_all), f32),
        pltpu.VMEM((d_all, own), bf16),
        pltpu.VMEM((zn, tok, own), bf16),
        pltpu.VMEM((zn, tok, own), bf16),
        pltpu.VMEM((zn, tok, own), bf16),
        pltpu.VMEM((d_all, d_all), bf16),
        pltpu.VMEM((2, nar, own), bf16),
        pltpu.VMEM((own, tok), bf16),
        pltpu.VMEM((tok, own), bf16),
        pltpu.VMEM((tok, own), f32),
        pltpu.VMEM((n, 8, own), f32),
        pltpu.VMEM((8, own), f32),
        pltpu.VMEM((zn, 8, own), f32),
        pltpu.VMEM((n, rp, d_all), bf16),
        pltpu.VMEM((n, rp, d_all), bf16),
        pltpu.VMEM((zn, rp, own), bf16),
        pltpu.VMEM((zn, rp, own), bf16),
        pltpu.VMEM((rp, d_all), bf16),
        pltpu.VMEM((h, 2, rp, d_all), bf16),
        pltpu.VMEM((2 * nar, d_all), bf16),
        pltpu.VMEM((nar, own), f32),
        pltpu.VMEM((nar, own), bf16),
        pltpu.VMEM((zn, nar, own), bf16),
        pltpu.VMEM((nar, d_all), f32),
        pltpu.VMEM((nar, d_all), bf16),
        pltpu.VMEM((nar, own), bf16),
        pltpu.VMEM((h, 2, nar, own), bf16),
        pltpu.VMEM((d_all, own), bf16),
    ]
    dma = pltpu.SemaphoreType.DMA
    scratch += [dma((5,)), dma((2,)), dma((2, 2, half, CHUNKS)), dma((1,)), dma((2, half)), dma((2,))]
    scratch += [dma((1,)), dma((zn,)), dma((1,)), dma((zn,)), dma((2,)), dma((2,)), dma((2,))]
    scratch += [dma((2, 2)), dma((2, 2)), dma((2, 3)), dma((2, 3)), dma((2,))]
    hbm = pl.BlockSpec(memory_space=pl.ANY)
    return pl.pallas_call(
        functools.partial(body, n, zn, row_count),
        out_shape=jax.ShapeDtypeStruct((tok, own), bf16),
        in_specs=[hbm] * 5,
        out_specs=VMEM,
        scratch_shapes=scratch,
        compiler_params=pltpu.CompilerParams(collective_id=1, has_side_effects=True, vmem_limit_bytes=58 * 2**20),
        cost_estimate=pl.CostEstimate(flops=8_000_000_000, bytes_accessed=16 * 2**20, transcendentals=0),
    )(features, grad_out, eigvecs.T, eigvals.reshape(1, d_all), whiten)


def solution(mesh):
    in_specs = (P("rows", "feat"), P("rows", "feat"), P("feat", "rows"), P(), P(None, "feat"))
    out_specs = P("rows", "feat")
    return jax.shard_map(local, mesh=mesh, in_specs=in_specs, out_specs=out_specs, check_vma=False)
```

time: 135 us -> 118 us (0.87)
  Pallas kernels: 130 us -> 116 us
  local copies, waits for them, and re-layouts: 4.17 us -> 1.87 us
    pallas_call x1, Pallas kernels: 130 us -> 116 us  [local(): pl.pallas_call(functools.partial(body, n, zn, row_count), out_shape=jax.S...]
    unnamed x4 -> x1, local copies, waits for them, and re-layouts: 4.15 us -> 1.87 us
where the time goes in v2:
time: 118 us
  Pallas kernels  116 us (98%)
  local copies, waits for them, and re-layouts  1.87 us (2%)
    pallas_call x1, Pallas kernels, local(): pl.pallas_call(functools.partial(body, n, zn, row_count), out_shape=jax.S...  116 us

profile of v2, /device:TPU:1, one launch (start us, length us, event | category | flops | bytes accessed | tf_op | source)
XLA Modules:
  0.0 117.9 jit_solution(3311254559381345497)
XLA Ops:
  0.0 116.0 %shard_map.55 = bf16[1024,256]{1,0:T(8,128)(2,1)} custom-call(bf16[1024,256]{1,0:T(8,128)(2,1)} %x_hbm.1, bf16[1024,256]{1,0:T(8,128)(2,1)} %g_hbm.1, f32[64,256]{1,0:T(8,128)} %bitcast.2, f32[1,2048]{1,0:T(1,128)} %bitcast.3, bf16[2048,256]{1,0:T(8,128)(2,1)} %w_hbm.1), custom_call_target="tpu_custom_call" | custom-call | flops 8000000000 | bytes 16777216 | tf_op jit(solution)/shard_map/pallas_call | solution.py:500
  116.0 1.9 %copy.7 = bf16[1024,256]{1,0:T(8,128)(2,1)} copy(bf16[1024,256]{1,0:T(8,128)(2,1)} %shard_map.55) | data formatting | bytes 1048576

commit v3 on v2

--- a/solution.py
+++ b/solution.py
@@ -11,7 +11,7 @@
 MESH = pl.DeviceIdType.MESH
 VMEM = pl.BlockSpec(memory_space=pltpu.VMEM)
 bf16, f32 = jnp.bfloat16, jnp.float32
-CHUNKS = 4
+CHUNKS = (4, 8)
 
 
 def remote(src, dst, send, recv, axis, target):
@@ -37,9 +37,9 @@
 
 
 def body(n, zn, row_count, x_hbm, g_hbm, v_hbm, e_hbm, w_hbm, o_ref,
-         x_ref, g_ref, v_ref, e_ref, w_ref, x_all, xc_all, g_all, v_all, v_pair, xct, gc, acc, sums, sums_own, means,
+         x_ref, g_ref, v_ref, e_ref, w_ref, x_all, xc_all, g_all, v_all, v_col, v_pair, xct, gc, acc, sums, sums_own, means,
          pieces, parts, tile, rtile, spiece, sall, vct, yacc, yown, yall, kern, mt, town, tall, sens,
-         ld, ring_s, ring_r, vr_s, vr_r, vm, v1_s, v1_r, v2_s, v2_r, vd, su, me_sem, rs_sem, sy_sem, ag_sem, am_sem, ya_sem):
+         ld, ring_s, ring_g, ring_x, vr_s, vr_r, vm, v1_s, v1_r, v2_s, v2_r, vd, vo, su, me_sem, rs_sem, sy_sem, ag_sem, am_sem, ya_sem):
     me, z = lax.axis_index("rows"), lax.axis_index("feat")
     core, chip = lax.rem(me, 2), me // 2
     mate = me + 1 - 2 * core
@@ -54,9 +54,9 @@
     wide = 2 * nar
     hv = own // 2
     rp = own // n
-    ck = tok // CHUNKS
     order = slot_order(zn)
-    every = list(range(CHUNKS))
+    ring_r = (ring_g, ring_x)
+
     loads = []
     for i, (src, dst) in enumerate([(g_hbm, g_ref), (v_hbm, v_ref), (x_hbm, x_ref), (e_hbm, e_ref), (w_hbm, w_ref)]):
         load = pltpu.make_async_copy(src, dst, ld.at[i])
@@ -87,19 +87,26 @@
     def next_of(way):
         return at_z(1) if way == 0 else at_z(zn - 1)
 
-    def units(step, way):
-        if step < half - 1:
-            return every
-        return every[: CHUNKS // 2] if way == 0 else every[CHUNKS // 2:]
+    def units(arr, step):
+        return range(CHUNKS[arr] if step < half - 1 else CHUNKS[arr] // 2)
 
     def hop(arr, way, step, unit):
         full, mine = (g_all, g_ref) if arr == 0 else (x_all, x_ref)
-        there = full.at[block_of(way, step), pl.ds(unit * ck, ck)]
-        src = there if step else mine.at[pl.ds(unit * ck, ck)]
-        return remote(src, there, ring_s.at[arr], ring_r.at[arr, way, step, unit], "feat", next_of(way))
+        count = CHUNKS[arr]
+        rows = pl.ds((unit + way * (count // 2)) % count * (tok // count), tok // count)
+        there = full.at[block_of(way, step), rows]
+        src = there if step else mine.at[rows]
+        return remote(src, there, ring_s.at[arr], ring_r[arr].at[way, step, unit], "feat", next_of(way))
 
     def vpart(block, lane):
         return v_all.at[rows_of(2 * block + core, hv), lanes(lane, wide)]
+
+    def v_mine(block):
+        return v_col.at[rows_of(2 * block + core, hv)]
+
+    def v_keep(block):
+        rows = rows_of(2 * block + core, hv)
+        v_all[rows, lanes(chip, wide)] = v_col[rows]
 
     def v_arrived(count, sem):
         if count * wide > d_all:
@@ -108,7 +115,7 @@
             arrived(v_all.at[pl.ds(0, hv), pl.ds(0, count * wide)], sem)
 
     def vhop(way, step):
-        ref = vpart(block_of(way, step), chip)
+        ref = v_mine(block_of(way, step))
         return remote(ref, ref, vr_s.at[0], vr_r.at[way, step], "feat", next_of(way))
 
     def y_first(rel):
@@ -121,18 +128,22 @@
         return (yy * nx + lax.rem(xx + d, nx)) * 2 + core
 
     def v_first(rel):
-        ref = vpart(at_z(rel), chip)
+        src, ref = v_mine(at_z(rel)), vpart(at_z(rel), chip)
+        if rel:
+            remote(src, src, vo.at[0], vo.at[1], "rows", mate).start()
+        v_keep(at_z(rel))
         for d in range(1, ny if y_first(rel) else nx):
             target = by_y(d) if y_first(rel) else by_x(d)
-            remote(ref, ref, v1_s.at[0], v1_r.at[rel], "rows", target).start()
+            remote(src, ref, v1_s.at[0], v1_r.at[rel], "rows", target).start()
 
     def v_second(rel):
         v_arrived((ny if y_first(rel) else nx) - 1, v1_r.at[rel])
         if y_first(rel):
             for e in range(ny):
                 ref = vpart(at_z(rel), lax.rem(yy + ny - e, ny) * nx + xx)
+                src = ref if e else v_mine(at_z(rel))
                 for d in range(1, nx):
-                    remote(ref, ref, v2_s.at[0], v2_r.at[rel], "rows", by_x(d)).start()
+                    remote(src, ref, v2_s.at[0], v2_r.at[rel], "rows", by_x(d)).start()
         else:
             ref = v_all.at[rows_of(2 * at_z(rel) + core, hv), lanes(yy, nx * wide)]
             for d in range(1, ny):
@@ -142,8 +153,9 @@
         v_arrived(ny * (nx - 1) if y_first(rel) else nx * (ny - 1), v2_r.at[rel])
         ref = v_all.at[rows_of(2 * at_z(rel) + core, hv)]
         remote(ref, ref, vd.at[0], vd.at[1], "rows", mate).start()
+
     for way in (0, 1):
-        hop(0, way, 0, units(0, way)[0]).start()
+        hop(0, way, 0, 0).start()
     pair = remote(v_pair.at[core], v_pair.at[core], vm.at[0], vm.at[1], "rows", mate)
     pair.start()
     loads[2].wait()
@@ -152,16 +164,17 @@
     sums_own[1:2] = jnp.sum(g_ref[...].astype(f32), axis=0, keepdims=True)
     pair.wait_recv()
     both = jnp.concatenate([v_pair[0].astype(f32), v_pair[1].astype(f32)], axis=0)
-    v_all[rows_of(z, own), lanes(chip, wide)] = both.T.astype(bf16)
+    v_col[rows_of(z, own)] = both.T.astype(bf16)
     for way in (0, 1):
         if way == 0 or half > 1:
             vhop(way, 0).start()
-        for unit in units(0, way)[1:]:
+        for unit in units(0, 0)[1:]:
             hop(0, way, 0, unit).start()
     for d in range(1, n):
         remote(sums_own, sums.at[me], su.at[0], su.at[1], "rows", lax.rem(me + d, n)).start()
     sums[me] = sums_own[...]
     v_first(0)
+
     loads[3].wait()
     root = jnp.sqrt(e_ref[...])
     shape = (nar, d_all)
@@ -169,6 +182,7 @@
     hit = wanted == lax.broadcasted_iota(jnp.int32, shape, 1)
     root_row = jnp.sum(jnp.where(hit, jnp.broadcast_to(root, shape), 0.0), axis=1, keepdims=True)
     kern[...] = -1.0 / ((root_row * root) * (root_row + root))
+
     arrived(sums.at[pl.ds(0, n - 1)], su.at[1])
     means[z] = jnp.sum(sums[...], axis=0) / row_count
     for d in range(1, zn):
@@ -205,7 +219,8 @@
         acc[...] = gw if slot == 0 else acc[...] + gw
 
     split = max(1, zn - 3)
-    groups = [(0, split), (split, zn)]
+    groups = [(lo, hi) for lo, hi in ((0, split), (split, zn - 1), (zn - 1, zn)) if lo < hi]
+    last = len(groups) - 1
     group_lanes = [pl.ds(lo * own, (hi - lo) * own) for lo, hi in groups]
 
     def rs_start(group):
@@ -270,7 +285,7 @@
             done.add((arr, way, step, unit))
             hop(arr, way, step, unit).wait_recv()
 
-    forwards = [(step, unit) for step in range(1, half) for unit in every]
+    forwards = [(step, unit) for step in range(half) for unit in units(1, step)]
     state = {"next": 0}
 
     def pump(count):
@@ -279,20 +294,22 @@
                 step, unit = forwards[state["next"]]
                 state["next"] += 1
                 for way in (0, 1):
-                    if unit in units(step, way):
+                    if step:
                         take(1, way, step - 1, unit)
-                        hop(1, way, step, unit).start()
+                    hop(1, way, step, unit).start()
 
     def all_in(arr, dist):
-        for unit in every:
+        for unit in units(arr, dist - 1):
             for way in (0, 1):
-                if unit in units(dist - 1, way):
-                    take(arr, way, dist - 1, unit)
+                take(arr, way, dist - 1, unit)
 
     def center(rel):
         q = at_z(rel)
         xc_all[q] = (x_all[q].astype(f32) - means[q, 0:1]).astype(bf16)
+
     gram(0)
+    if split == 1:
+        rs_start(0)
     product(0)
     v_second(0)
     rels = [[0]]
@@ -307,65 +324,64 @@
                 v_first(rel)
                 got.append(rel)
         rels.append(got)
-        for unit in every:
+        for unit in units(0, dist - 1):
             for way in (0, 1):
-                if unit in units(dist - 1, way):
-                    take(0, way, dist - 1, unit)
-                    if dist < half and unit in units(dist, way):
-                        hop(0, way, dist, unit).start()
-            if dist < half and unit == 1:
-                for rel in rels[dist - 1]:
+                take(0, way, dist - 1, unit)
+                if dist < half and unit in units(0, dist):
+                    hop(0, way, dist, unit).start()
+            if dist == half - 1 and unit >= CHUNKS[0] // 2:
+                pump(2)
+            if dist == half:
+                pump(2 - unit)
+            if dist >= 2 and unit == 1:
+                for rel in rels[dist - 2]:
                     v_third(rel)
-            if dist < half and unit == 2:
-                for rel in rels[dist]:
-                    v_second(rel)
-        if dist == half - 1 or half == 1:
-            for unit in every:
-                for way in (0, 1):
-                    if unit in units(0, way):
-                        hop(1, way, 0, unit).start()
         if dist == 1:
             arrived(means.at[pl.ds(0, zn - 1)], me_sem.at[1])
         mine = [slot for slot in range(zn) if order[slot] in (dist, zn - dist)]
-        if dist == 1 and split == 1:
-            rs_start(0)
         for slot in mine:
             gram(slot)
+            for group in range(last):
+                if slot == groups[group][1] - 1:
+                    rs_start(group)
             if dist < half:
                 product(slot)
-            if slot == split - 1:
-                rs_start(0)
         if dist == half - 1:
             rs_sum(0)
             sym_start(0)
-    rs_start(1)
+        if dist < half - 1:
+            for rel in rels[dist]:
+                v_second(rel)
+    rs_start(last)
     product(zn - 1)
-    if half == 1:
-        rs_sum(0)
-        sym_start(0)
-    sym_end(0)
-    sall[chip, core, :, group_lanes[0]] = spiece[:, group_lanes[0]]
-    gather_start(0, spiece.at[:, group_lanes[0]], s_view(0))
+    for group in range(1 if half > 1 else 0, last):
+        rs_sum(group)
+        sym_start(group)
+    pump(1)
     if half > 1:
         for rel in rels[half - 1]:
-            v_third(rel)
-    else:
-        v_third(0)
-    pump(1)
+            v_second(rel)
+    pump(2)
+    rs_sum(last)
+    sym_start(last)
+    pump(2)
+
+    def s_start(group):
+        sym_end(group)
+        lane = group_lanes[group]
+        sall[chip, core, :, lane] = spiece[:, lane]
+        gather_start(group, spiece.at[:, lane], s_view(group))
+
+    for group in range(last):
+        s_start(group)
     for rel in rels[half]:
         v_second(rel)
-    rs_sum(1)
-    sym_start(1)
     pump(2)
-    passes = [gather_pass(0, s_view(0))]
-    for rel in rels[half]:
-        v_third(rel)
+    s_start(last)
     pump(1)
-    sym_end(1)
-    sall[chip, core, :, group_lanes[1]] = spiece[:, group_lanes[1]]
-    gather_start(1, spiece.at[:, group_lanes[1]], s_view(1))
-    arrived(v_all.at[pl.ds(0, d_all // 2)], vd.at[1])
-    vct[...] = v_all[:, lanes(chip, wide)].astype(f32).T.astype(bf16)
+    passes = [gather_pass(group, s_view(group)) for group in range(last)]
+    v_arrived(zn - 1, vo.at[1])
+    vct[...] = v_col[...].astype(f32).T.astype(bf16)
     yacc[...] = jnp.zeros_like(yacc)
 
     def y_part(group):
@@ -386,40 +402,50 @@
                 def _():
                     yacc[...] += mm(left, block, 1, 1)
 
-    y_part(0)
+    for group in range(last):
+        y_part(group)
     pump(2)
-    passes.append(gather_pass(1, s_view(1)))
-    y_part(1)
+    passes.append(gather_pass(last, s_view(last)))
+    y_part(last)
     yown[...] = yacc[...].astype(bf16)
     for d in range(1, zn):
         remote(yown, yall.at[z], ya_sem.at[0], ya_sem.at[1], "feat", at_z(d)).start()
     yall[z] = yown[...]
-    pump(2)
+    for rel in rels[half - 1] + rels[half]:
+        v_third(rel)
+    pump(1)
     if half > 1:
         all_in(1, 1)
         center(zn - 1)
         center(1)
     arrived(yall.at[pl.ds(0, zn - 1)], ya_sem.at[1])
+    arrived(v_all.at[pl.ds(0, d_all // 2)], vd.at[1])
     left = jnp.concatenate([yall[q] for q in range(zn)], axis=1)
     mt[...] = (kern[...] * mm(left, v_all[...])).astype(bf16)
     town[...] = mm(mt[...], v_all[rows_of(z, own)], 1, 1).astype(bf16)
     tall[chip, core] = town[...]
-    gather_start(2, town, t_view)
-    pump(len(forwards))
+    gather_start(3, town, t_view)
+    pump(6)
     if half > 2:
         all_in(1, 2)
         center(zn - 2)
         center(2)
-    passes.append(gather_pass(2, t_view))
-    passes[2].wait_recv()
-    @pl.loop(0, zn)
+    passes.append(gather_pass(3, t_view))
+    pump(2)
+    passes[-1].wait_recv()
+    pump(len(forwards))
+
+    step_rows = d_all // 4
+
+    @pl.loop(0, 4)
     def _(q):
-        part = mm(v_all[rows_of(q, own)], tall[...].reshape(d_all, own))
-        sens[rows_of(q, own)] = ((2.0 / row_count) * part).astype(bf16)
+        part = mm(v_all[rows_of(q, step_rows)], tall[...].reshape(d_all, own))
+        sens[rows_of(q, step_rows)] = ((2.0 / row_count) * part).astype(bf16)
 
     def finish(rel):
         q = at_z(rel)
         acc[...] += mm(xc_all[q], sens[rows_of(q, own)])
+
     finish(0)
     for dist in range(1, half):
         if dist > 2:
@@ -432,6 +458,7 @@
     center(half)
     q = at_z(half)
     o_ref[...] = (acc[...] + mm(xc_all[q], sens[rows_of(q, own)])).astype(bf16)
+
     pair.wait_send()
     for arr, full in ((0, g_all), (1, x_all)):
         arrived(full.at[pl.ds(0, zn - 1)], ring_s.at[arr])
@@ -439,14 +466,15 @@
     v_arrived(sum((ny if y_first(rel) else nx) - 1 for rel in range(zn)), v1_s.at[0])
     v_arrived(sum(ny * (nx - 1) if y_first(rel) else nx * (ny - 1) for rel in range(zn)), v2_s.at[0])
     arrived(v_all.at[pl.ds(0, d_all // 2)], vd.at[0])
+    v_arrived(zn - 1, vo.at[0])
     arrived(sums.at[pl.ds(0, n - 1)], su.at[0])
     arrived(means.at[pl.ds(0, zn - 1)], me_sem.at[0])
-    for group in range(2):
+    for group in range(last + 1):
         arrived(parts.at[pl.ds(0, n - 1), :, group_lanes[group]], rs_sem.at[0, group])
         if len(sym_slots(group)):
             arrived(sym_bytes(group), sy_sem.at[0, group])
         arrived(s_view(group)(pl.ds(0, h - 1), core), ag_sem.at[0, group])
-    arrived(t_view(pl.ds(0, h - 1), core), ag_sem.at[0, 2])
+    arrived(t_view(pl.ds(0, h - 1), core), ag_sem.at[0, 3])
     for copy in passes:
         copy.wait_send()
     arrived(yall.at[pl.ds(0, zn - 1)], ya_sem.at[0])
@@ -469,6 +497,7 @@
         pltpu.VMEM((zn, tok, own), bf16),
         pltpu.VMEM((zn, tok, own), bf16),
         pltpu.VMEM((d_all, d_all), bf16),
+        pltpu.VMEM((d_all, 2 * nar), bf16),
         pltpu.VMEM((2, nar, own), bf16),
         pltpu.VMEM((own, tok), bf16),
         pltpu.VMEM((tok, own), bf16),
@@ -493,9 +522,9 @@
         pltpu.VMEM((d_all, own), bf16),
     ]
     dma = pltpu.SemaphoreType.DMA
-    scratch += [dma((5,)), dma((2,)), dma((2, 2, half, CHUNKS)), dma((1,)), dma((2, half)), dma((2,))]
-    scratch += [dma((1,)), dma((zn,)), dma((1,)), dma((zn,)), dma((2,)), dma((2,)), dma((2,))]
-    scratch += [dma((2, 2)), dma((2, 2)), dma((2, 3)), dma((2, 3)), dma((2,))]
+    scratch += [dma((5,)), dma((2,)), dma((2, half, CHUNKS[0])), dma((2, half, CHUNKS[1])), dma((1,)), dma((2, half)), dma((2,))]
+    scratch += [dma((1,)), dma((zn,)), dma((1,)), dma((zn,)), dma((2,)), dma((2,)), dma((2,)), dma((2,))]
+    scratch += [dma((2, 3)), dma((2, 3)), dma((2, 4)), dma((2, 4)), dma((2,))]
     hbm = pl.BlockSpec(memory_space=pl.ANY)
     return pl.pallas_call(
         functools.partial(body, n, zn, row_count),

time: 118 us -> 111 us (0.941)
  Pallas kernels: 116 us -> 109 us
    pallas_call x1, Pallas kernels: 116 us -> 109 us  [local(): pl.pallas_call(functools.partial(body, n, zn, row_count), out_shape=jax.S...]
where the time goes in v3:
time: 111 us
  Pallas kernels  109 us (98%)
  local copies, waits for them, and re-layouts  1.87 us (2%)
    pallas_call x1, Pallas kernels, local(): pl.pallas_call(functools.partial(body, n, zn, row_count), out_shape=jax.S...  109 us

profile of v3, /device:TPU:1, one launch (start us, length us, event | category | flops | bytes accessed | tf_op | source)
XLA Modules:
  0.0 111.2 jit_solution(11161812174716582662)
XLA Ops:
  0.0 109.3 %shard_map.55 = bf16[1024,256]{1,0:T(8,128)(2,1)} custom-call(bf16[1024,256]{1,0:T(8,128)(2,1)} %x_hbm.1, bf16[1024,256]{1,0:T(8,128)(2,1)} %g_hbm.1, f32[64,256]{1,0:T(8,128)} %bitcast.2, f32[1,2048]{1,0:T(1,128)} %bitcast.3, bf16[2048,256]{1,0:T(8,128)(2,1)} %w_hbm.1), custom_call_target="tpu_custom_call" | custom-call | flops 8000000000 | bytes 16777216 | tf_op jit(solution)/shard_map/pallas_call | solution.py:529
  109.3 1.9 %copy.7 = bf16[1024,256]{1,0:T(8,128)(2,1)} copy(bf16[1024,256]{1,0:T(8,128)(2,1)} %shard_map.55) | data formatting | bytes 1048576

commit v4 on v3

--- a/solution.py
+++ b/solution.py
@@ -329,10 +329,13 @@
                 take(0, way, dist - 1, unit)
                 if dist < half and unit in units(0, dist):
                     hop(0, way, dist, unit).start()
-            if dist == half - 1 and unit >= CHUNKS[0] // 2:
+            if dist == half - 1 and unit == 1:
+                rs_sum(0)
+                sym_start(0)
+            if dist == half - 1 and unit == 3:
                 pump(2)
             if dist == half:
-                pump(2 - unit)
+                pump(1)
             if dist >= 2 and unit == 1:
                 for rel in rels[dist - 2]:
                     v_third(rel)
@@ -346,39 +349,38 @@
                     rs_start(group)
             if dist < half:
                 product(slot)
-        if dist == half - 1:
-            rs_sum(0)
-            sym_start(0)
         if dist < half - 1:
             for rel in rels[dist]:
                 v_second(rel)
-    rs_start(last)
-    product(zn - 1)
-    for group in range(1 if half > 1 else 0, last):
-        rs_sum(group)
-        sym_start(group)
-    pump(1)
-    if half > 1:
-        for rel in rels[half - 1]:
-            v_second(rel)
-    pump(2)
-    rs_sum(last)
-    sym_start(last)
-    pump(2)
-
     def s_start(group):
         sym_end(group)
         lane = group_lanes[group]
         sall[chip, core, :, lane] = spiece[:, lane]
         gather_start(group, spiece.at[:, lane], s_view(group))
 
-    for group in range(last):
+    rs_start(last)
+    product(zn - 1)
+    if half == 1:
+        rs_sum(0)
+        sym_start(0)
+    s_start(0)
+    if half > 1:
+        for rel in rels[half - 1]:
+            v_second(rel)
+    for group in range(1, last):
+        rs_sum(group)
+        sym_start(group)
+    pump(2)
+    rs_sum(last)
+    sym_start(last)
+    pump(2)
+    for group in range(1, last):
         s_start(group)
+    pump(2)
+    s_start(last)
     for rel in rels[half]:
         v_second(rel)
-    pump(2)
-    s_start(last)
-    pump(1)
+    pump(4)
     passes = [gather_pass(group, s_view(group)) for group in range(last)]
     v_arrived(zn - 1, vo.at[1])
     vct[...] = v_col[...].astype(f32).T.astype(bf16)
@@ -404,7 +406,7 @@
 
     for group in range(last):
         y_part(group)
-    pump(2)
+    pump(1)
     passes.append(gather_pass(last, s_view(last)))
     y_part(last)
     yown[...] = yacc[...].astype(bf16)
@@ -413,28 +415,28 @@
     yall[z] = yown[...]
     for rel in rels[half - 1] + rels[half]:
         v_third(rel)
-    pump(1)
+    pump(2)
     if half > 1:
         all_in(1, 1)
         center(zn - 1)
         center(1)
     arrived(yall.at[pl.ds(0, zn - 1)], ya_sem.at[1])
+    pump(4)
     arrived(v_all.at[pl.ds(0, d_all // 2)], vd.at[1])
     left = jnp.concatenate([yall[q] for q in range(zn)], axis=1)
     mt[...] = (kern[...] * mm(left, v_all[...])).astype(bf16)
     town[...] = mm(mt[...], v_all[rows_of(z, own)], 1, 1).astype(bf16)
     tall[chip, core] = town[...]
     gather_start(3, town, t_view)
-    pump(6)
+    pump(4)
     if half > 2:
         all_in(1, 2)
         center(zn - 2)
         center(2)
+    pump(2)
     passes.append(gather_pass(3, t_view))
-    pump(2)
+    pump(len(forwards))
     passes[-1].wait_recv()
-    pump(len(forwards))
-
     step_rows = d_all // 4
 
     @pl.loop(0, 4)
@@ -528,7 +530,7 @@
     hbm = pl.BlockSpec(memory_space=pl.ANY)
     return pl.pallas_call(
         functools.partial(body, n, zn, row_count),
-        out_shape=jax.ShapeDtypeStruct((tok, own), bf16),
+        out_shape=pltpu.VMEM((tok, own), bf16),
         in_specs=[hbm] * 5,
         out_specs=VMEM,
         scratch_shapes=scratch,

time: 111 us -> 105 us (0.946)
  Pallas kernels: 109 us -> 104 us
    pallas_call x1, Pallas kernels: 109 us -> 104 us  [local(): pl.pallas_call(functools.partial(body, n, zn, row_count), out_shape=pltpu...]
where the time goes in v4:
time: 105 us
  Pallas kernels  104 us (99%)
    pallas_call x1, Pallas kernels, local(): pl.pallas_call(functools.partial(body, n, zn, row_count), out_shape=pltpu...  104 us

profile of v4, /device:TPU:1, one launch (start us, length us, event | category | flops | bytes accessed | tf_op | source)
XLA Modules:
  0.0 105.1 jit_solution(4140764874628290941)
XLA Ops:
  0.0 104.3 %shard_map.55 = bf16[1024,256]{1,0:T(8,128)(2,1)S(1)} custom-call(bf16[1024,256]{1,0:T(8,128)(2,1)} %x_hbm.1, bf16[1024,256]{1,0:T(8,128)(2,1)} %g_hbm.1, f32[64,256]{1,0:T(8,128)} %bitcast.2, f32[1,2048]{1,0:T(1,128)} %bitcast.3, bf16[2048,256]{1,0:T(8,128)(2,1)} %w_hbm.1), custom_call_target="tpu_custom_call" | custom-call | flops 8000000000 | bytes 16777216 | tf_op jit(solution)/shard_map/pallas_call | solution.py:531
  104.3 0.8 copy.7

commit v5 on v4

--- a/solution.py
+++ b/solution.py
@@ -11,7 +11,7 @@
 MESH = pl.DeviceIdType.MESH
 VMEM = pl.BlockSpec(memory_space=pltpu.VMEM)
 bf16, f32 = jnp.bfloat16, jnp.float32
-CHUNKS = (4, 8)
+CHUNKS = (4, 4)
 
 
 def remote(src, dst, send, recv, axis, target):
@@ -159,7 +159,6 @@
     pair = remote(v_pair.at[core], v_pair.at[core], vm.at[0], vm.at[1], "rows", mate)
     pair.start()
     loads[2].wait()
-    sums_own[...] = jnp.zeros_like(sums_own)
     sums_own[0:1] = jnp.sum(x_ref[...].astype(f32), axis=0, keepdims=True)
     sums_own[1:2] = jnp.sum(g_ref[...].astype(f32), axis=0, keepdims=True)
     pair.wait_recv()
@@ -333,9 +332,9 @@
                 rs_sum(0)
                 sym_start(0)
             if dist == half - 1 and unit == 3:
-                pump(2)
+                pump(1)
             if dist == half:
-                pump(1)
+                pump(1 - unit)
             if dist >= 2 and unit == 1:
                 for rel in rels[dist - 2]:
                     v_third(rel)
@@ -370,18 +369,18 @@
     for group in range(1, last):
         rs_sum(group)
         sym_start(group)
-    pump(2)
+    pump(1)
     rs_sum(last)
     sym_start(last)
-    pump(2)
+    pump(1)
+    passes = [gather_pass(0, s_view(0))] if last else []
     for group in range(1, last):
         s_start(group)
-    pump(2)
+    pump(1)
     s_start(last)
     for rel in rels[half]:
         v_second(rel)
-    pump(4)
-    passes = [gather_pass(group, s_view(group)) for group in range(last)]
+    pump(2)
     v_arrived(zn - 1, vo.at[1])
     vct[...] = v_col[...].astype(f32).T.astype(bf16)
     yacc[...] = jnp.zeros_like(yacc)
@@ -404,36 +403,40 @@
                 def _():
                     yacc[...] += mm(left, block, 1, 1)
 
-    for group in range(last):
+    if last:
+        y_part(0)
+    for group in range(1, last + 1):
+        passes.append(gather_pass(group, s_view(group)))
+    if not last:
+        passes.append(gather_pass(0, s_view(0)))
+    pump(1)
+    for group in range(1 if last else 0, last + 1):
         y_part(group)
-    pump(1)
-    passes.append(gather_pass(last, s_view(last)))
-    y_part(last)
     yown[...] = yacc[...].astype(bf16)
     for d in range(1, zn):
         remote(yown, yall.at[z], ya_sem.at[0], ya_sem.at[1], "feat", at_z(d)).start()
     yall[z] = yown[...]
     for rel in rels[half - 1] + rels[half]:
         v_third(rel)
-    pump(2)
+    pump(1)
     if half > 1:
         all_in(1, 1)
         center(zn - 1)
         center(1)
     arrived(yall.at[pl.ds(0, zn - 1)], ya_sem.at[1])
-    pump(4)
+    pump(2)
     arrived(v_all.at[pl.ds(0, d_all // 2)], vd.at[1])
     left = jnp.concatenate([yall[q] for q in range(zn)], axis=1)
     mt[...] = (kern[...] * mm(left, v_all[...])).astype(bf16)
     town[...] = mm(mt[...], v_all[rows_of(z, own)], 1, 1).astype(bf16)
     tall[chip, core] = town[...]
     gather_start(3, town, t_view)
-    pump(4)
+    pump(2)
     if half > 2:
         all_in(1, 2)
         center(zn - 2)
         center(2)
-    pump(2)
+    pump(1)
     passes.append(gather_pass(3, t_view))
     pump(len(forwards))
     passes[-1].wait_recv()
@@ -504,9 +507,9 @@
         pltpu.VMEM((own, tok), bf16),
         pltpu.VMEM((tok, own), bf16),
         pltpu.VMEM((tok, own), f32),
-        pltpu.VMEM((n, 8, own), f32),
-        pltpu.VMEM((8, own), f32),
-        pltpu.VMEM((zn, 8, own), f32),
+        pltpu.VMEM((n, 2, own), f32),
+        pltpu.VMEM((2, own), f32),
+        pltpu.VMEM((zn, 2, own), f32),
         pltpu.VMEM((n, rp, d_all), bf16),
         pltpu.VMEM((n, rp, d_all), bf16),
         pltpu.VMEM((zn, rp, own), bf16),

time: 105 us -> 104 us (level)
    pallas_call x1, Pallas kernels: 104 us -> 103 us  [local(): pl.pallas_call(functools.partial(body, n, zn, row_count), out_shape=pltpu...]
where the time goes in v5:
time: 104 us
  Pallas kernels  103 us (99%)
    pallas_call x1, Pallas kernels, local(): pl.pallas_call(functools.partial(body, n, zn, row_count), out_shape=pltpu...  103 us

profile of v5, /device:TPU:1, one launch (start us, length us, event | category | flops | bytes accessed | tf_op | source)
XLA Modules:
  0.0 103.8 jit_solution(9051502748947770519)
XLA Ops:
  0.0 103.0 %shard_map.55 = bf16[1024,256]{1,0:T(8,128)(2,1)S(1)} custom-call(bf16[1024,256]{1,0:T(8,128)(2,1)} %x_hbm.1, bf16[1024,256]{1,0:T(8,128)(2,1)} %g_hbm.1, f32[64,256]{1,0:T(8,128)} %bitcast.2, f32[1,2048]{1,0:T(1,128)} %bitcast.3, bf16[2048,256]{1,0:T(8,128)(2,1)} %w_hbm.1), custom_call_target="tpu_custom_call" | custom-call | flops 8000000000 | bytes 16777216 | tf_op jit(solution)/shard_map/pallas_call | solution.py:534
  103.0 0.8 copy.7

commit v6 on v5

--- a/solution.py
+++ b/solution.py
@@ -38,8 +38,8 @@
 
 def body(n, zn, row_count, x_hbm, g_hbm, v_hbm, e_hbm, w_hbm, o_ref,
          x_ref, g_ref, v_ref, e_ref, w_ref, x_all, xc_all, g_all, v_all, v_col, v_pair, xct, gc, acc, sums, sums_own, means,
-         pieces, parts, tile, rtile, spiece, sall, vct, yacc, yown, yall, kern, mt, town, tall, sens,
-         ld, ring_s, ring_g, ring_x, vr_s, vr_r, vm, v1_s, v1_r, v2_s, v2_r, vd, vo, su, me_sem, rs_sem, sy_sem, ag_sem, am_sem, ya_sem):
+         pieces, parts, tile, rtile, spiece, sall, vct, yacc, yown, yall, kern, mt, tout, tin, town, tall, sens, xv, xvb,
+         ld, ring_s, ring_g, ring_x, vr_s, vr_r, vm, v1_s, v1_r, v2_s, v2_r, vd, vo, su, me_sem, rs_sem, sy_sem, ag_sem, am_sem, ya_sem, tz_sem):
     me, z = lax.axis_index("rows"), lax.axis_index("feat")
     core, chip = lax.rem(me, 2), me // 2
     mate = me + 1 - 2 * core
@@ -176,8 +176,8 @@
 
     loads[3].wait()
     root = jnp.sqrt(e_ref[...])
-    shape = (nar, d_all)
-    wanted = me * nar + lax.broadcasted_iota(jnp.int32, shape, 0)
+    shape = (nar // zn, d_all)
+    wanted = me * nar + z * (nar // zn) + lax.broadcasted_iota(jnp.int32, shape, 0)
     hit = wanted == lax.broadcasted_iota(jnp.int32, shape, 1)
     root_row = jnp.sum(jnp.where(hit, jnp.broadcast_to(root, shape), 0.0), axis=1, keepdims=True)
     kern[...] = -1.0 / ((root_row * root) * (root_row + root))
@@ -409,13 +409,13 @@
         passes.append(gather_pass(group, s_view(group)))
     if not last:
         passes.append(gather_pass(0, s_view(0)))
-    pump(1)
+    pump(0)
     for group in range(1 if last else 0, last + 1):
         y_part(group)
-    yown[...] = yacc[...].astype(bf16)
+    yown[...] = yacc[...].reshape(zn, nar // zn, own).astype(bf16)
     for d in range(1, zn):
-        remote(yown, yall.at[z], ya_sem.at[0], ya_sem.at[1], "feat", at_z(d)).start()
-    yall[z] = yown[...]
+        remote(yown.at[at_z(d)], yall.at[z], ya_sem.at[0], ya_sem.at[1], "feat", at_z(d)).start()
+    yall[z] = yown[z]
     for rel in rels[half - 1] + rels[half]:
         v_third(rel)
     pump(1)
@@ -423,46 +423,59 @@
         all_in(1, 1)
         center(zn - 1)
         center(1)
+
+    def early(rels, first, final):
+        rows_each = tok // 4
+
+        @pl.loop(0, 4)
+        def _(i):
+            rows = rows_of(i, rows_each)
+            total = 0.0 if first else xv[rows]
+            for rel in rels:
+                q = at_z(rel)
+                total = total + mm(xc_all[q, rows], v_all[rows_of(q, own)])
+            if final:
+                xvb[rows] = total.astype(bf16)
+            else:
+                xv[rows] = total
+
     arrived(yall.at[pl.ds(0, zn - 1)], ya_sem.at[1])
-    pump(2)
+    pump(1)
     arrived(v_all.at[pl.ds(0, d_all // 2)], vd.at[1])
     left = jnp.concatenate([yall[q] for q in range(zn)], axis=1)
     mt[...] = (kern[...] * mm(left, v_all[...])).astype(bf16)
-    town[...] = mm(mt[...], v_all[rows_of(z, own)], 1, 1).astype(bf16)
+    t_rows = mm(mt[...], v_all[...], 1, 1)
+    for q in range(zn):
+        tout[q] = t_rows[:, q * own:(q + 1) * own].astype(bf16)
+    for d in range(1, zn):
+        remote(tout.at[at_z(d)], tin.at[z], tz_sem.at[0], tz_sem.at[1], "feat", at_z(d)).start()
+    tin[z] = tout[z]
+    pump(2)
+    early([0, zn - 1, 1] if half > 1 else [0], True, half <= 2)
+    arrived(tin.at[pl.ds(0, zn - 1)], tz_sem.at[1])
+    town[...] = tin[...].astype(f32).reshape(nar, own).astype(bf16)
     tall[chip, core] = town[...]
     gather_start(3, town, t_view)
     pump(2)
-    if half > 2:
-        all_in(1, 2)
-        center(zn - 2)
-        center(2)
-    pump(1)
-    passes.append(gather_pass(3, t_view))
+    for dist in range(2, half):
+        if dist == half - 1:
+            passes.append(gather_pass(3, t_view))
+        all_in(1, dist)
+        center(zn - dist)
+        center(dist)
+        early([zn - dist, dist], False, dist == half - 1)
+        pump(1)
+    if half <= 2:
+        passes.append(gather_pass(3, t_view))
     pump(len(forwards))
     passes[-1].wait_recv()
-    step_rows = d_all // 4
-
-    @pl.loop(0, 4)
-    def _(q):
-        part = mm(v_all[rows_of(q, step_rows)], tall[...].reshape(d_all, own))
-        sens[rows_of(q, step_rows)] = ((2.0 / row_count) * part).astype(bf16)
-
-    def finish(rel):
-        q = at_z(rel)
-        acc[...] += mm(xc_all[q], sens[rows_of(q, own)])
-
-    finish(0)
-    for dist in range(1, half):
-        if dist > 2:
-            all_in(1, dist)
-            center(zn - dist)
-            center(dist)
-        finish(zn - dist)
-        finish(dist)
+    scale = 2.0 / row_count
+    acc[...] += scale * mm(xvb[...], tall[...].reshape(d_all, own))
+    last_rows = rows_of(at_z(half), own)
+    sens[...] = (scale * mm(v_all[last_rows], tall[...].reshape(d_all, own))).astype(bf16)
     all_in(1, half)
     center(half)
-    q = at_z(half)
-    o_ref[...] = (acc[...] + mm(xc_all[q], sens[rows_of(q, own)])).astype(bf16)
+    o_ref[...] = (acc[...] + mm(xc_all[at_z(half)], sens[...])).astype(bf16)
 
     pair.wait_send()
     for arr, full in ((0, g_all), (1, x_all)):
@@ -483,6 +496,7 @@
     for copy in passes:
         copy.wait_send()
     arrived(yall.at[pl.ds(0, zn - 1)], ya_sem.at[0])
+    arrived(tin.at[pl.ds(0, zn - 1)], tz_sem.at[0])
 
 
 def local(features, grad_out, eigvecs, eigvals, whiten):
@@ -518,18 +532,22 @@
         pltpu.VMEM((h, 2, rp, d_all), bf16),
         pltpu.VMEM((2 * nar, d_all), bf16),
         pltpu.VMEM((nar, own), f32),
-        pltpu.VMEM((nar, own), bf16),
-        pltpu.VMEM((zn, nar, own), bf16),
-        pltpu.VMEM((nar, d_all), f32),
-        pltpu.VMEM((nar, d_all), bf16),
+        pltpu.VMEM((zn, nar // zn, own), bf16),
+        pltpu.VMEM((zn, nar // zn, own), bf16),
+        pltpu.VMEM((nar // zn, d_all), f32),
+        pltpu.VMEM((nar // zn, d_all), bf16),
+        pltpu.VMEM((zn, nar // zn, own), bf16),
+        pltpu.VMEM((zn, nar // zn, own), bf16),
         pltpu.VMEM((nar, own), bf16),
         pltpu.VMEM((h, 2, nar, own), bf16),
-        pltpu.VMEM((d_all, own), bf16),
+        pltpu.VMEM((own, own), bf16),
+        pltpu.VMEM((tok, d_all), f32),
+        pltpu.VMEM((tok, d_all), bf16),
     ]
     dma = pltpu.SemaphoreType.DMA
     scratch += [dma((5,)), dma((2,)), dma((2, half, CHUNKS[0])), dma((2, half, CHUNKS[1])), dma((1,)), dma((2, half)), dma((2,))]
     scratch += [dma((1,)), dma((zn,)), dma((1,)), dma((zn,)), dma((2,)), dma((2,)), dma((2,)), dma((2,))]
-    scratch += [dma((2, 3)), dma((2, 3)), dma((2, 4)), dma((2, 4)), dma((2,))]
+    scratch += [dma((2, 3)), dma((2, 3)), dma((2, 4)), dma((2, 4)), dma((2,)), dma((2,))]
     hbm = pl.BlockSpec(memory_space=pl.ANY)
     return pl.pallas_call(
         functools.partial(body, n, zn, row_count),

time: 104 us -> 102 us (0.981)
  Pallas kernels: 103 us -> 101 us
    pallas_call x1, Pallas kernels: 103 us -> 101 us  [local(): pl.pallas_call(functools.partial(body, n, zn, row_count), out_shape=pltpu...]
where the time goes in v6:
time: 102 us
  Pallas kernels  101 us (99%)
    pallas_call x1, Pallas kernels, local(): pl.pallas_call(functools.partial(body, n, zn, row_count), out_shape=pltpu...  101 us

profile of v6, /device:TPU:1, one launch (start us, length us, event | category | flops | bytes accessed | tf_op | source)
XLA Modules:
  0.0 102.1 jit_solution(12122650472690349613)
XLA Ops:
  0.0 101.3 %shard_map.55 = bf16[1024,256]{1,0:T(8,128)(2,1)S(1)} custom-call(bf16[1024,256]{1,0:T(8,128)(2,1)} %x_hbm.1, bf16[1024,256]{1,0:T(8,128)(2,1)} %g_hbm.1, f32[64,256]{1,0:T(8,128)} %bitcast.2, f32[1,2048]{1,0:T(1,128)} %bitcast.3, bf16[2048,256]{1,0:T(8,128)(2,1)} %w_hbm.1), custom_call_target="tpu_custom_call" | custom-call | flops 8000000000 | bytes 16777216 | tf_op jit(solution)/shard_map/pallas_call | solution.py:552
  101.3 0.8 copy.7

commit v7 on v6

--- a/solution.py
+++ b/solution.py
@@ -463,7 +463,7 @@
         all_in(1, dist)
         center(zn - dist)
         center(dist)
-        early([zn - dist, dist], False, dist == half - 1)
+        early([zn - dist, dist] if dist < half - 1 else [zn - dist], False, dist == half - 1)
         pump(1)
     if half <= 2:
         passes.append(gather_pass(3, t_view))
@@ -471,11 +471,15 @@
     passes[-1].wait_recv()
     scale = 2.0 / row_count
     acc[...] += scale * mm(xvb[...], tall[...].reshape(d_all, own))
-    last_rows = rows_of(at_z(half), own)
-    sens[...] = (scale * mm(v_all[last_rows], tall[...].reshape(d_all, own))).astype(bf16)
+    late = [half - 1, half] if half > 2 else [half]
+    for i, rel in enumerate(late):
+        part = mm(v_all[rows_of(at_z(rel), own)], tall[...].reshape(d_all, own))
+        sens[i] = (scale * part).astype(bf16)
+    for i, rel in enumerate(late[:-1]):
+        acc[...] += mm(xc_all[at_z(rel)], sens[i])
     all_in(1, half)
     center(half)
-    o_ref[...] = (acc[...] + mm(xc_all[at_z(half)], sens[...])).astype(bf16)
+    o_ref[...] = (acc[...] + mm(xc_all[at_z(half)], sens[len(late) - 1])).astype(bf16)
 
     pair.wait_send()
     for arr, full in ((0, g_all), (1, x_all)):
@@ -540,7 +544,7 @@
         pltpu.VMEM((zn, nar // zn, own), bf16),
         pltpu.VMEM((nar, own), bf16),
         pltpu.VMEM((h, 2, nar, own), bf16),
-        pltpu.VMEM((own, own), bf16),
+        pltpu.VMEM((2, own, own), bf16),
         pltpu.VMEM((tok, d_all), f32),
         pltpu.VMEM((tok, d_all), bf16),
     ]

time: 102 us -> 102 us (level)
  no operation moved by 1% of the time
where the time goes in v7:
time: 102 us
  Pallas kernels  101 us (99%)
    pallas_call x1, Pallas kernels, local(): pl.pallas_call(functools.partial(body, n, zn, row_count), out_shape=pltpu...  101 us

profile of v7, /device:TPU:1, one launch (start us, length us, event | category | flops | bytes accessed | tf_op | source)
XLA Modules:
  0.0 102.3 jit_solution(15467586153771245731)
XLA Ops:
  0.0 101.5 %shard_map.55 = bf16[1024,256]{1,0:T(8,128)(2,1)S(1)} custom-call(bf16[1024,256]{1,0:T(8,128)(2,1)} %x_hbm.1, bf16[1024,256]{1,0:T(8,128)(2,1)} %g_hbm.1, f32[64,256]{1,0:T(8,128)} %bitcast.2, f32[1,2048]{1,0:T(1,128)} %bitcast.3, bf16[2048,256]{1,0:T(8,128)(2,1)} %w_hbm.1), custom_call_target="tpu_custom_call" | custom-call | flops 8000000000 | bytes 16777216 | tf_op jit(solution)/shard_map/pallas_call | solution.py:556
  101.5 0.8 copy.7
